TPU v7x, 256 devices: a whole 4x4x8 slice. The times are simulated.
256 devices in a mesh: gx: 4 (over x), gz: 64 (over z, y, core).
Axes of the slice: x: 4, y: 4, z: 8, core: 2. Of those that a mesh axis runs over, the one named last changes fastest.
Arguments:
- velocity: float32 [3, 64, 256, 512], P(None, 'gz', None, 'gx'), may hold values from -3.5 to 3.5
- earlier_term: bfloat16 [3, 64, 256, 512], P(None, 'gz', None, 'gx'), may hold values from -4 to 4
- face_metric: float32 [2, 64], replicated, may hold values from 0.5 to 2, as said below
Outputs:
- new_velocity: float32 [3, 64, 256, 512], P(None, 'gz', None, 'gx')
- pressure: float32 [64, 256, 512], P('gz', None, 'gx')
Inputs may be any that keep to these rules, and one draw needn't show every extreme that they name: face_metric[1, k] equals face_metric[0, k + 1].
All inputs are finite; a program needn't handle non-finite values.
Results may differ from a plain program's by a relative error of at most 0.0012.
Values sent between devices are 32-bit elements; how exact they have to be, the bound alone decides.
A program may use at most 64 MiB of HBM per device.

v0:
```python
import math

import jax
import jax.numpy as jnp
from jax import lax
from jax.sharding import PartitionSpec as P

TIME_STEP = 0.4
ADVECT_WEIGHT = 5.0 / 12.0
EARLIER_WEIGHT = -17.0 / 60.0
VISCOUS_WEIGHT = 2.0 / 15.0


def padded(cells, sides, width, closed):
    for axis, dim in sides:
        count = lax.axis_size(axis)
        ends = count if closed else count - 1
        head = lax.slice_in_dim(cells, 0, width, axis=dim)
        tail = lax.slice_in_dim(cells, cells.shape[dim] - width, cells.shape[dim], axis=dim)
        cells = jnp.concatenate(
            [
                lax.ppermute(tail, axis, [(i, (i + 1) % count) for i in range(ends)]),
                cells,
                lax.ppermute(head, axis, [((i + 1) % count, i) for i in range(ends)]),
            ],
            axis=dim,
        )
    return cells


def cosine_table(extent):
    wavenumber = jnp.arange(extent, dtype=jnp.int32)[:, None]
    points = jnp.arange(extent, dtype=jnp.int32)[None, :]
    residue = wavenumber * (2 * points + 1) % (4 * extent)
    cosines = jnp.cos(residue.astype(jnp.float32) * (math.pi / (2 * extent))) * math.sqrt(
        2.0 / extent
    )
    return cosines.at[0].multiply(math.sqrt(0.5))


def wave_squares(extent):
    return (jnp.arange(extent, dtype=jnp.float32) * (math.pi / extent)) ** 2


def transform_y(cosines, field):
    return jnp.einsum("jy,zyx->zjx", cosines, field, precision=lax.Precision.HIGHEST)


def inverse_y(cosines, field):
    return jnp.einsum("jy,zjx->zyx", cosines, field, precision=lax.Precision.HIGHEST)


def neighbours_y(field):
    y_after = jnp.concatenate([field[..., 1:, :], field[..., -1:, :]], -2)
    y_before = jnp.concatenate([field[..., :1, :], field[..., :-1, :]], -2)
    return (y_after, y_before)


def compose_rows(earlier, latter):
    early_p, early_q, early_r, early_t, early_u, early_v = earlier
    late_p, late_q, late_r, late_t, late_u, late_v = latter
    new_p = late_p * early_p + late_q * early_r
    new_q = late_p * early_q + late_q
    new_r = late_r * early_p + early_r
    new_s = late_r * early_q + 1.0
    new_t = late_t * early_p + late_u * early_r + late_v * early_t
    new_u = late_t * early_q + late_u + late_v * early_u
    new_v = late_v * early_v
    inverse_s = 1.0 / new_s
    return (
        new_p * inverse_s,
        new_q * inverse_s,
        new_r * inverse_s,
        new_t * inverse_s,
        new_u * inverse_s,
        new_v * inverse_s,
    )


def compose_maps(earlier, latter):
    return (latter[0] + latter[1] * earlier[0], latter[1] * earlier[1])


def row_elements(diagonal, lower_face, upper_face, scaled):
    zeros_part = jnp.zeros_like(diagonal)
    lower_ratio = -lower_face / diagonal
    return (
        zeros_part,
        upper_face / diagonal,
        lower_ratio,
        zeros_part,
        scaled / diagonal,
        lower_ratio,
    )


def solve_whole(columns, eigen_local, lower_all, upper_all):
    metric = 0.5 * (lower_all + upper_all)
    diagonals = -(lower_all + upper_all) - eigen_local[None, :] / metric
    elements = row_elements(diagonals, lower_all, upper_all, columns / metric)
    forward = lax.associative_scan(compose_rows, elements, axis=0)
    maps_down = (forward[4][::-1], -forward[1][::-1])
    backward = lax.associative_scan(compose_maps, maps_down, axis=0)
    return backward[0][::-1]


def per_device(velocity, earlier_term, face_metric):
    z_cells = velocity.shape[1]
    height = velocity.shape[2]
    breadth = velocity.shape[3]
    groups = lax.axis_size("gx")
    layers_all = lax.axis_size("gz")
    length = breadth * groups
    y_band = height // groups
    layer_index = lax.axis_index("gz")
    own_faces = lax.dynamic_slice_in_dim(face_metric, layer_index * z_cells, z_cells, 1)
    lower_face = own_faces[0][:, None, None]
    upper_face = own_faces[1][:, None, None]
    metric = 0.5 * (lower_face + upper_face)
    y_cosines = cosine_table(height)
    y_squares = wave_squares(height)
    wide_x = padded(velocity, (("gx", 3),), 1, True)
    wide_z = padded(velocity, (("gz", 1),), 1, False)
    x_after = wide_x[..., 2:]
    x_before = wide_x[..., :-2]
    z_after = wide_z[:, 2:]
    z_before = wide_z[:, :-2]
    y_after, y_before = neighbours_y(velocity)
    grad_x = 0.5 * (x_after - x_before)
    grad_y = 0.5 * (y_after - y_before)
    grad_z = metric * (0.5 * (z_after - z_before))
    lap_x = x_after + x_before - 2.0 * velocity
    lap_z = metric * (upper_face * (z_after - velocity) - lower_face * (velocity - z_before))
    planes = velocity.reshape(3 * z_cells, height, breadth)
    lap_y = inverse_y(y_cosines, -y_squares[:, None] * transform_y(y_cosines, planes)).reshape(
        velocity.shape
    )
    advect = velocity[0:1] * grad_x + velocity[1:2] * grad_y + velocity[2:3] * grad_z
    predicted = velocity + TIME_STEP * (
        -ADVECT_WEIGHT * advect
        + EARLIER_WEIGHT * earlier_term.astype(jnp.float32)
        + VISCOUS_WEIGHT * (lap_x + lap_y + lap_z)
    )
    pred_x = padded(predicted[0], (("gx", 2),), 1, True)
    pred_z = padded(predicted[2], (("gz", 0),), 1, False)
    v_after, v_before = neighbours_y(predicted[1])
    divergence = (
        0.5 * (pred_x[..., 2:] - pred_x[..., :-2])
        + 0.5 * (v_after - v_before)
        + metric * (0.5 * (pred_z[2:] - pred_z[:-2]))
    )
    source = divergence / TIME_STEP
    y_coeffs = transform_y(y_cosines, source)
    grouped = lax.all_to_all(y_coeffs, "gx", split_axis=1, concat_axis=2, tiled=True)
    x_cosines = cosine_table(length)
    coeffs = lax.dot_general(
        grouped.reshape(-1, length),
        x_cosines,
        (((1,), (1,)), ((), ())),
        precision=lax.Precision.HIGHEST,
    ).reshape(z_cells, y_band * length)
    band_squares = lax.dynamic_slice_in_dim(y_squares, lax.axis_index("gx") * y_band, y_band, 0)
    eigen_sum = (band_squares[:, None] + wave_squares(length)[None, :]).reshape(-1)
    modes_local = y_band * length // layers_all
    columns = lax.all_to_all(coeffs, "gz", split_axis=1, concat_axis=0, tiled=True)
    eigen_local = lax.dynamic_slice_in_dim(eigen_sum, layer_index * modes_local, modes_local, 0)
    whole_solved = solve_whole(
        columns, eigen_local, face_metric[0][:, None], face_metric[1][:, None]
    )
    solved = lax.all_to_all(whole_solved, "gz", split_axis=0, concat_axis=1, tiled=True)
    physical_x = lax.dot_general(
        solved.reshape(-1, length),
        x_cosines,
        (((1,), (0,)), ((), ())),
        precision=lax.Precision.HIGHEST,
    ).reshape(z_cells, y_band, length)
    spread = lax.all_to_all(physical_x, "gx", split_axis=2, concat_axis=1, tiled=True)
    pressure = inverse_y(y_cosines, spread)
    wide_p = padded(pressure, (("gx", 2),), 1, True)
    press_x = 0.5 * (wide_p[..., 2:] - wide_p[..., :-2])
    wall_p = padded(pressure, (("gz", 0),), 1, False)
    p_after, p_before = neighbours_y(pressure)
    press_y = 0.5 * (p_after - p_before)
    press_z = metric * (0.5 * (wall_p[2:] - wall_p[:-2]))
    new_velocity = predicted - TIME_STEP * jnp.stack([press_x, press_y, press_z])
    return (new_velocity, pressure)


def solution(mesh):
    placed = (P(None, "gz", None, "gx"), P(None, "gz", None, "gx"), P())
    return jax.shard_map(
        per_device,
        mesh=mesh,
        in_specs=placed,
        out_specs=(P(None, "gz", None, "gx"), P("gz", None, "gx")),
        check_vma=False,
    )
```

profile of v0, /device:TPU:1, one launch (start us, length us, event | category | flops | bytes accessed | tf_op | source)
XLA Modules:
  0.0 124.1 jit_solution(11466830301117513914)
XLA Ops:
  0.6 1.2 copy.107
  1.9 5.1 %collective-permute-start.2 = (f32[3,1,256,128]{2,3,0,1:T(8,128)S(1)}, f32[3,1,256,128]{2,3,0,1:T(8,128)}, u32[]{:S(2)}, u32[]{:S(2)}) collective-permute-start(f32[3,1,256,128]{2,3,0,1:T(8,128)S(1)} %copy.107), channel_id=1, source_target_pairs={{1,0},{2,1},{3,2},{4,3},{5,4},{6,5},{7,6},{8,7},{9,8},{10,9},{11,1... | collective-permute-start | bytes 1179656 | tf_op jit(solution)/shard_map/ppermute | solution.py:24
  7.0 1.9 %collective-permute-start.3 = (f32[3,1,256,128]{2,3,0,1:T(8,128)S(1)}, f32[3,1,256,128]{2,3,0,1:T(8,128)}, u32[]{:S(2)}, u32[]{:S(2)}) collective-permute-start(f32[3,1,256,128]{2,3,0,1:T(8,128)S(1)} %copy.107), channel_id=1, source_target_pairs={{0,1},{1,2},{2,3},{3,4},{4,5},{5,6},{6,7},{7,8},{8,9},{9,10},{10,1... | collective-permute-start | bytes 1179656 | tf_op jit(solution)/shard_map/ppermute | solution.py:22
  8.9 0.6 fusion.103
  9.5 2.0 %collective-permute-start = (f32[3,1,256,1]{2,3,0,1:T(1,128)}, f32[3,1,256,1]{2,3,0,1:T(1,128)S(1)}, u32[]{:S(2)}, u32[]{:S(2)}) collective-permute-start(f32[3,1,256,1]{2,3,0,1:T(1,128)} %get-tuple-element.45), channel_id=1, source_target_pairs={{64,0},{128,64},{192,128},{0,192},{65,1},{129,65},{193,129},{1,193... | collective-permute-start | bytes 9224 | tf_op jit(solution)/shard_map/ppermute | solution.py:24
  11.5 0.7 multiply_bitcast_fusion.2
  12.2 1.0 fusion.23
  13.3 3.8 %fusion.5 = f32[512,512]{1,0:T(8,128)S(1)} fusion(s32[512]{0:T(512)S(1)} %multiply_add_fusion.5), kind=kLoop, calls=%fused_computation.13 | loop fusion | flops 3932160 | bytes 1050624 | tf_op jit(solution)/shard_map/mul | solution.py:35
  17.1 0.6 fusion
  17.7 0.1 dynamic_slice.10
  17.8 0.7 add_bitcast_fusion
  18.6 0.2 fusion.105
  18.7 0.6 fusion.119
  19.3 0.1 copy-done.2
  19.5 0.8 copy.93
  20.2 0.8 copy.98
  21.0 0.8 copy.99
  21.7 0.1 copy.95
  21.9 0.8 copy.97
  22.7 0.8 copy.102
  24.8 3.8 %fusion.16 = f32[3,1,256,128]{2,3,0,1:T(8,128)S(1)} fusion(f32[3,1,256,128]{2,3,0,1:T(8,128)S(1)} %copy.107, f32[3,1,1,128]{2,3,0,1:T(8,128)S(1)} %copy.95, f32[3,1,255,128]{2,3,0,1:T(8,128)S(1)} %get-tuple-element.49, f32[3,1,255,128]{2,3,0,1:T(8,128)S(1)} %get-tuple-element.48, f32[3,1,1,128]{2,3,0,1:T(8,128)} %copy.97, ...), kind=kOutput, calls=%fused_computation.27 | convolution fusion | flops 305135616 | bytes 3610640 | tf_op jit(solution)/shard_map/jy,zjx->zyx/dot_general | solution.py:50
  28.7 3.2 %collective-permute-start.6 = (f32[1,256,128]{1,2,0:T(8,128)S(1)}, f32[1,256,128]{1,2,0:T(8,128)S(1)}, u32[]{:S(2)}, u32[]{:S(2)}) collective-permute-start(f32[1,256,128]{1,2,0:T(8,128)S(1)} %get-tuple-element.38), channel_id=1, source_target_pairs={{1,0},{2,1},{3,2},{4,3},{5,4},{6,5},{7,6},{8,7},{9,8},{10,9},{11,1... | collective-permute-start | bytes 393224 | tf_op jit(solution)/shard_map/ppermute | solution.py:24
  31.9 2.4 %collective-permute-start.7 = (f32[1,256,128]{1,2,0:T(8,128)S(1)}, f32[1,256,128]{1,2,0:T(8,128)S(1)}, u32[]{:S(2)}, u32[]{:S(2)}) collective-permute-start(f32[1,256,128]{1,2,0:T(8,128)S(1)} %get-tuple-element.38), channel_id=1, source_target_pairs={{0,1},{1,2},{2,3},{3,4},{4,5},{5,6},{6,7},{7,8},{8,9},{9,10},{10,1... | collective-permute-start | bytes 393224 | tf_op jit(solution)/shard_map/ppermute | solution.py:22
  34.3 0.1 fusion.110
  34.4 2.8 %collective-permute-start.4 = (f32[1,256,1]{1,2,0:T(1,128)S(1)}, f32[1,256,1]{1,2,0:T(1,128)S(1)}, u32[]{:S(2)}, u32[]{:S(2)}) collective-permute-start(f32[1,256,1]{1,2,0:T(1,128)S(1)} %get-tuple-element.73), channel_id=1, source_target_pairs={{64,0},{128,64},{192,128},{0,192},{65,1},{129,65},{193,129},{1,193... | collective-permute-start | bytes 3080 | tf_op jit(solution)/shard_map/ppermute | solution.py:24
  37.2 0.6 collective-permute-done.4
  37.9 2.9 %collective-permute-done.5 = f32[1,256,1]{1,2,0:T(1,128)S(1)} collective-permute-done((f32[1,256,1]{1,2,0:T(1,128)S(1)}, f32[1,256,1]{1,2,0:T(1,128)S(1)}, u32[]{:S(2)}, u32[]{:S(2)}) %collective-permute-start.5) | collective-permute-done | bytes 1056 | tf_op jit(solution)/shard_map/ppermute | solution.py:22
  40.8 0.4 convolution_bitcast_fusion.2
  41.2 0.8 copy.111
  42.0 3.3 %all-to-all-start = ((f32[1,256,128]{2,0,1:T(1,128)}), f32[1,256,128]{2,0,1:T(1,128)S(1)}, u32[]{:S(2)}, u32[]{:S(2)}) async-start(f32[1,256,128]{2,0,1:T(1,128)} %copy.111), calls=%async_computation | async-start | bytes 262144 | tf_op jit(solution)/shard_map/all_to_all | solution.py:154
  45.3 0.2 scatter-mul.9
  45.6 4.5 %all-to-all-done = f32[1,256,128]{2,0,1:T(1,128)S(1)} async-done(((f32[1,256,128]{2,0,1:T(1,128)}), f32[1,256,128]{2,0,1:T(1,128)S(1)}, u32[]{:S(2)}, u32[]{:S(2)}) %all-to-all-start) | async-done | bytes 131104 | tf_op jit(solution)/shard_map/all_to_all | solution.py:154
  50.1 0.1 copy.112
  50.2 1.1 convolution_bitcast_fusion.3
  51.3 0.8 copy.113
  52.1 16.5 %all-to-all-start.1 = ((f32[1,64,512]{2,0,1:T(1,128)}), f32[1,64,512]{2,0,1:T(1,128)S(1)}, u32[]{:S(2)}, u32[]{:S(2)}) async-start(f32[1,64,512]{2,0,1:T(1,128)} %copy.113), calls=%async_computation.1 | async-start | bytes 262144 | tf_op jit(solution)/shard_map/all_to_all | solution.py:165
  68.8 10.9 %all-to-all-done.1 = f32[1,64,512]{2,0,1:T(1,128)S(1)} async-done(((f32[1,64,512]{2,0,1:T(1,128)}), f32[1,64,512]{2,0,1:T(1,128)S(1)}, u32[]{:S(2)}, u32[]{:S(2)}) %all-to-all-start.1) | async-done | bytes 131104 | tf_op jit(solution)/shard_map/all_to_all | solution.py:165
  79.7 0.1 bitcast_divide_fusion
  82.7 0.1 rev.7
  83.1 0.1 slice.775
  83.2 0.1 slice.778
  84.4 0.1 slice.770
  84.7 0.1 rev.8
  84.8 0.1 copy.114
  84.9 14.9 %all_to_all.59 = f32[64,1,512]{2,1,0:T(1,128)S(1)} all-to-all(f32[64,1,512]{2,1,0:T(1,128)S(1)} %copy.114), channel_id=1, replica_groups=mesh['gx'=4,'gz'=64] {'gz'}, dimensions={0} | all-to-all | bytes 262144 | tf_op jit(solution)/shard_map/all_to_all | solution.py:170
  99.8 1.8 %fusion.52 = f32[64,512]{0,1:T(8,128)S(1)} fusion(f32[512,512]{1,0:T(8,128)S(1)} %scatter-mul.9, f32[64,1,512]{2,1,0:T(1,128)S(1)} %all_to_all.59), kind=kOutput, calls=%fused_computation.74 | convolution fusion | flops 201326592 | bytes 1310720 | tf_op jit(solution)/shard_map/dot_general | solution.py:171
  101.6 0.5 broadcast.369
  102.1 1.3 %reduce.4 = f32[512,64]{1,0:T(8,128)S(1)} reduce(f32[512,1,64]{2,1,0:T(1,128)S(1)} %bitcast.105, f32[]{:T(128)} %broadcast.369), dimensions={1}, to_apply=%bitcast.95.reduce_sub_computation | reduce | bytes 262148
  103.4 0.2 reshape.453
  103.6 7.2 %all_to_all.60 = f32[4,1,8192]{2,1,0:T(1,128)S(1)} all-to-all(f32[4,1,8192]{2,1,0:T(1,128)S(1)} %reshape.453), channel_id=1, replica_groups=mesh['gx'=4,'gz'=64] {'gx'}, dimensions={0} | all-to-all | bytes 262144 | tf_op jit(solution)/shard_map/all_to_all | solution.py:177
  110.9 1.0 reduce.5
  111.8 0.3 reshape.454
  112.2 0.1 copy.116
  112.3 0.4 convolution_bitcast_fusion.1
  112.7 0.1 fusion.108
  112.8 0.1 fusion.107
  112.9 3.4 %collective-permute-start.10 = (f32[1,256,128]{1,2,0:T(8,128)S(1)}, f32[1,256,128]{1,2,0:T(8,128)S(1)}, u32[]{:S(2)}, u32[]{:S(2)}) collective-permute-start(f32[1,256,128]{1,2,0:T(8,128)S(1)} %convolution_bitcast_fusion.1), channel_id=1, source_target_pairs={{1,0},{2,1},{3,2},{4,3},{5,4},{6,5},{7,6},{8,7},{9,8},{10,9},{11,1... | collective-permute-start | bytes 393224 | tf_op jit(solution)/shard_map/ppermute | solution.py:24
  116.4 2.1 %collective-permute-start.11 = (f32[1,256,128]{1,2,0:T(8,128)S(1)}, f32[1,256,128]{1,2,0:T(8,128)S(1)}, u32[]{:S(2)}, u32[]{:S(2)}) collective-permute-start(f32[1,256,128]{1,2,0:T(8,128)S(1)} %convolution_bitcast_fusion.1), channel_id=1, source_target_pairs={{0,1},{1,2},{2,3},{3,4},{4,5},{5,6},{6,7},{7,8},{8,9},{9,10},{10,1... | collective-permute-start | bytes 393224 | tf_op jit(solution)/shard_map/ppermute | solution.py:22
  118.5 1.0 collective-permute-start.8
  119.5 0.6 collective-permute-start.9
  120.0 0.1 fusion.51
  120.2 0.8 copy.121
  121.0 2.1 %collective-permute-done.9 = f32[1,256,1]{1,2,0:T(1,128)S(1)} collective-permute-done((f32[1,256,1]{1,2,0:T(1,128)S(1)}, f32[1,256,1]{1,2,0:T(1,128)S(1)}, u32[]{:S(2)}, u32[]{:S(2)}) %collective-permute-start.9) | collective-permute-done | bytes 1056 | tf_op jit(solution)/shard_map/ppermute | solution.py:22
  123.2 0.9 copy.120
  (243 shorter events, 4.2 us)
Async XLA Ops:
  0.6 10.9 %copy-start = (f32[3,1,256,128]{3,2,1,0:T(8,128)S(1)}, f32[3,1,256,128]{3,2,1,0:T(8,128)}, u32[]{:S(2)}) copy-start(f32[3,1,256,128]{3,2,1,0:T(8,128)} %param.7) | copy-start | bytes 1179652
  1.9 22.9 %collective-permute-start.2 = (f32[3,1,256,128]{2,3,0,1:T(8,128)S(1)}, f32[3,1,256,128]{2,3,0,1:T(8,128)}, u32[]{:S(2)}, u32[]{:S(2)}) collective-permute-start(f32[3,1,256,128]{2,3,0,1:T(8,128)S(1)} %copy.107), channel_id=1, source_target_pairs={{1,0},{2,1},{3,2},{4,3},{5,4},{6,5},{7,6},{8,7},{9,8},{10,9},{11,1... | collective-permute-start | bytes 1179656 | tf_op jit(solution)/shard_map/ppermute | solution.py:24
  7.0 17.8 %collective-permute-start.3 = (f32[3,1,256,128]{2,3,0,1:T(8,128)S(1)}, f32[3,1,256,128]{2,3,0,1:T(8,128)}, u32[]{:S(2)}, u32[]{:S(2)}) collective-permute-start(f32[3,1,256,128]{2,3,0,1:T(8,128)S(1)} %copy.107), channel_id=1, source_target_pairs={{0,1},{1,2},{2,3},{3,4},{4,5},{5,6},{6,7},{7,8},{8,9},{9,10},{10,1... | collective-permute-start | bytes 1179656 | tf_op jit(solution)/shard_map/ppermute | solution.py:22
  9.5 15.3 %collective-permute-start = (f32[3,1,256,1]{2,3,0,1:T(1,128)}, f32[3,1,256,1]{2,3,0,1:T(1,128)S(1)}, u32[]{:S(2)}, u32[]{:S(2)}) collective-permute-start(f32[3,1,256,1]{2,3,0,1:T(1,128)} %get-tuple-element.45), channel_id=1, source_target_pairs={{64,0},{128,64},{192,128},{0,192},{65,1},{129,65},{193,129},{1,193... | collective-permute-start | bytes 9224 | tf_op jit(solution)/shard_map/ppermute | solution.py:24
  11.5 13.3 %collective-permute-start.1 = (f32[3,1,256,1]{2,3,0,1:T(1,128)}, f32[3,1,256,1]{2,3,0,1:T(1,128)}, u32[]{:S(2)}, u32[]{:S(2)}) collective-permute-start(f32[3,1,256,1]{2,3,0,1:T(1,128)} %get-tuple-element.44), channel_id=1, source_target_pairs={{0,64},{64,128},{128,192},{192,0},{1,65},{65,129},{129,193},{193,1... | collective-permute-start | bytes 9224 | tf_op jit(solution)/shard_map/ppermute | solution.py:22
  17.8 0.7 copy-start.4
  18.6 0.9 copy-start.2
  21.7 1.0 copy-start.3
  28.7 12.1 %collective-permute-start.6 = (f32[1,256,128]{1,2,0:T(8,128)S(1)}, f32[1,256,128]{1,2,0:T(8,128)S(1)}, u32[]{:S(2)}, u32[]{:S(2)}) collective-permute-start(f32[1,256,128]{1,2,0:T(8,128)S(1)} %get-tuple-element.38), channel_id=1, source_target_pairs={{1,0},{2,1},{3,2},{4,3},{5,4},{6,5},{7,6},{8,7},{9,8},{10,9},{11,1... | collective-permute-start | bytes 393224 | tf_op jit(solution)/shard_map/ppermute | solution.py:24
  31.9 8.9 %collective-permute-start.7 = (f32[1,256,128]{1,2,0:T(8,128)S(1)}, f32[1,256,128]{1,2,0:T(8,128)S(1)}, u32[]{:S(2)}, u32[]{:S(2)}) collective-permute-start(f32[1,256,128]{1,2,0:T(8,128)S(1)} %get-tuple-element.38), channel_id=1, source_target_pairs={{0,1},{1,2},{2,3},{3,4},{4,5},{5,6},{6,7},{7,8},{8,9},{9,10},{10,1... | collective-permute-start | bytes 393224 | tf_op jit(solution)/shard_map/ppermute | solution.py:22
  34.4 3.5 %collective-permute-start.4 = (f32[1,256,1]{1,2,0:T(1,128)S(1)}, f32[1,256,1]{1,2,0:T(1,128)S(1)}, u32[]{:S(2)}, u32[]{:S(2)}) collective-permute-start(f32[1,256,1]{1,2,0:T(1,128)S(1)} %get-tuple-element.73), channel_id=1, source_target_pairs={{64,0},{128,64},{192,128},{0,192},{65,1},{129,65},{193,129},{1,193... | collective-permute-start | bytes 3080 | tf_op jit(solution)/shard_map/ppermute | solution.py:24
  37.1 3.6 %collective-permute-start.5 = (f32[1,256,1]{1,2,0:T(1,128)S(1)}, f32[1,256,1]{1,2,0:T(1,128)S(1)}, u32[]{:S(2)}, u32[]{:S(2)}) collective-permute-start(f32[1,256,1]{1,2,0:T(1,128)S(1)} %get-tuple-element.74), channel_id=1, source_target_pairs={{0,64},{64,128},{128,192},{192,0},{1,65},{65,129},{129,193},{193,1... | collective-permute-start | bytes 3080 | tf_op jit(solution)/shard_map/ppermute | solution.py:22
  42.0 8.1 %all-to-all-start = ((f32[1,256,128]{2,0,1:T(1,128)}), f32[1,256,128]{2,0,1:T(1,128)S(1)}, u32[]{:S(2)}, u32[]{:S(2)}) async-start(f32[1,256,128]{2,0,1:T(1,128)} %copy.111), calls=%async_computation | async-start | bytes 262144 | tf_op jit(solution)/shard_map/all_to_all | solution.py:154
  52.1 16.6 %copy-start.1 = (f32[8,4,8,128]{3,2,1,0:T(8,128)S(1)}, f32[8,4,8,128]{3,2,1,0:T(8,128)}, u32[]{:S(2)}) copy-start(f32[8,4,8,128]{3,2,1,0:T(8,128)} %add_bitcast_fusion) | copy-start | bytes 393220
  52.1 27.6 %all-to-all-start.1 = ((f32[1,64,512]{2,0,1:T(1,128)}), f32[1,64,512]{2,0,1:T(1,128)S(1)}, u32[]{:S(2)}, u32[]{:S(2)}) async-start(f32[1,64,512]{2,0,1:T(1,128)} %copy.113), calls=%async_computation.1 | async-start | bytes 262144 | tf_op jit(solution)/shard_map/all_to_all | solution.py:165
  112.9 10.2 %collective-permute-start.10 = (f32[1,256,128]{1,2,0:T(8,128)S(1)}, f32[1,256,128]{1,2,0:T(8,128)S(1)}, u32[]{:S(2)}, u32[]{:S(2)}) collective-permute-start(f32[1,256,128]{1,2,0:T(8,128)S(1)} %convolution_bitcast_fusion.1), channel_id=1, source_target_pairs={{1,0},{2,1},{3,2},{4,3},{5,4},{6,5},{7,6},{8,7},{9,8},{10,9},{11,1... | collective-permute-start | bytes 393224 | tf_op jit(solution)/shard_map/ppermute | solution.py:24
  116.4 6.8 %collective-permute-start.11 = (f32[1,256,128]{1,2,0:T(8,128)S(1)}, f32[1,256,128]{1,2,0:T(8,128)S(1)}, u32[]{:S(2)}, u32[]{:S(2)}) collective-permute-start(f32[1,256,128]{1,2,0:T(8,128)S(1)} %convolution_bitcast_fusion.1), channel_id=1, source_target_pairs={{0,1},{1,2},{2,3},{3,4},{4,5},{5,6},{6,7},{7,8},{8,9},{9,10},{10,1... | collective-permute-start | bytes 393224 | tf_op jit(solution)/shard_map/ppermute | solution.py:22
  118.5 2.5 %collective-permute-start.8 = (f32[1,256,1]{1,2,0:T(1,128)S(1)}, f32[1,256,1]{1,2,0:T(1,128)S(1)}, u32[]{:S(2)}, u32[]{:S(2)}) collective-permute-start(f32[1,256,1]{1,2,0:T(1,128)S(1)} %get-tuple-element.60), channel_id=1, source_target_pairs={{64,0},{128,64},{192,128},{0,192},{65,1},{129,65},{193,129},{1,193... | collective-permute-start | bytes 3080 | tf_op jit(solution)/shard_map/ppermute | solution.py:24
  119.5 3.6 %collective-permute-start.9 = (f32[1,256,1]{1,2,0:T(1,128)S(1)}, f32[1,256,1]{1,2,0:T(1,128)S(1)}, u32[]{:S(2)}, u32[]{:S(2)}) collective-permute-start(f32[1,256,1]{1,2,0:T(1,128)S(1)} %get-tuple-element.61), channel_id=1, source_target_pairs={{0,64},{64,128},{128,192},{192,0},{1,65},{65,129},{129,193},{193,1... | collective-permute-start | bytes 3080 | tf_op jit(solution)/shard_map/ppermute | solution.py:22
where the time goes:
time: 125 us; the launch traced here: 124 us
  starting transfers between devices  44.3 us (35%)
  blocking collectives  22.1 us (18%)
  waiting for transfers between devices  21.2 us (17%)
  local copies, waits for them, and re-layouts  15.6 us (12%)
  other arithmetic  9.72 us (8%)
  matrix products  8.15 us (7%)
  between operations  3.13 us (3%)
    ppermute x6, starting transfers between devices, padded(): lax.ppermute(head, axis, [((i + 1) % count, i) for i in range(ends)])  17.4 us
    all_to_all x1, starting transfers between devices, per_device(): lax.all_to_all(coeffs, 'gz', split_axis=1, concat_axis=0, tiled=True)  16.5 us
    all_to_all x1, blocking collectives, per_device(): lax.all_to_all(whole_solved, 'gz', split_axis=0, concat_axis=1, tiled=True)  14.9 us
    all_to_all x1, waiting for transfers between devices, per_device(): lax.all_to_all(coeffs, 'gz', split_axis=1, concat_axis=0, tiled=True)  10.9 us
    all_to_all x1, blocking collectives, per_device(): lax.all_to_all(physical_x, 'gx', split_axis=2, concat_axis=1, tiled=True)  7.22 us
    ppermute x6, starting transfers between devices, padded(): lax.ppermute(tail, axis, [(i, (i + 1) % count) for i in range(ends)])  6.99 us
    ppermute x6, waiting for transfers between devices, padded(): lax.ppermute(tail, axis, [(i, (i + 1) % count) for i in range(ends)])  5.01 us
    unnamed x18, local copies, waits for them, and re-layouts  4.93 us
  transfers between devices with their start and end apart: 14, of which 6 were waited for; matrix products, arithmetic and copies ran while one was open for 11% of the time, Pallas kernels for 0%

commit v1 on v0

--- a/solution.py
+++ b/solution.py
@@ -3,6 +3,8 @@
 import jax
 import jax.numpy as jnp
 from jax import lax
+from jax.experimental import pallas as pl
+from jax.experimental.pallas import tpu as pltpu
 from jax.sharding import PartitionSpec as P
 
 TIME_STEP = 0.4
@@ -56,52 +58,138 @@
     return (y_after, y_before)
 
 
-def compose_rows(earlier, latter):
-    early_p, early_q, early_r, early_t, early_u, early_v = earlier
-    late_p, late_q, late_r, late_t, late_u, late_v = latter
-    new_p = late_p * early_p + late_q * early_r
-    new_q = late_p * early_q + late_q
-    new_r = late_r * early_p + early_r
-    new_s = late_r * early_q + 1.0
-    new_t = late_t * early_p + late_u * early_r + late_v * early_t
-    new_u = late_t * early_q + late_u + late_v * early_u
-    new_v = late_v * early_v
-    inverse_s = 1.0 / new_s
-    return (
-        new_p * inverse_s,
-        new_q * inverse_s,
-        new_r * inverse_s,
-        new_t * inverse_s,
-        new_u * inverse_s,
-        new_v * inverse_s,
-    )
-
-
-def compose_maps(earlier, latter):
-    return (latter[0] + latter[1] * earlier[0], latter[1] * earlier[1])
-
-
-def row_elements(diagonal, lower_face, upper_face, scaled):
-    zeros_part = jnp.zeros_like(diagonal)
-    lower_ratio = -lower_face / diagonal
-    return (
-        zeros_part,
-        upper_face / diagonal,
-        lower_ratio,
-        zeros_part,
-        scaled / diagonal,
-        lower_ratio,
-    )
-
-
-def solve_whole(columns, eigen_local, lower_all, upper_all):
-    metric = 0.5 * (lower_all + upper_all)
-    diagonals = -(lower_all + upper_all) - eigen_local[None, :] / metric
-    elements = row_elements(diagonals, lower_all, upper_all, columns / metric)
-    forward = lax.associative_scan(compose_rows, elements, axis=0)
-    maps_down = (forward[4][::-1], -forward[1][::-1])
-    backward = lax.associative_scan(compose_maps, maps_down, axis=0)
-    return backward[0][::-1]
+LOGICAL = pl.DeviceIdType.LOGICAL
+
+
+def relative_devices(group, layer):
+    z_parts = [((layer & 56) + (shift << 3)) & 56 for shift in range(8)]
+    y_parts = [((layer & 6) + (shift << 1)) & 6 for shift in range(4)]
+    core_parts = [layer & 1, (layer & 1) ^ 1]
+    x_parts = [(group + shift) & 3 for shift in range(4)]
+    order = [
+        (i, j, k, m)
+        for j in (4, 3, 5, 2, 6, 1, 7, 0)
+        for k in (2, 1, 3, 0)
+        for i in (2, 1, 3, 0)
+        for m in (1, 0)
+    ]
+    return [
+        (x_parts[i], z_parts[j] | y_parts[k] | core_parts[m])
+        for i, j, k, m in order
+        if (i, j, k, m) != (0, 0, 0, 0)
+    ]
+
+
+def spectral_kernel(
+    faces,
+    y_rows,
+    x_cosines,
+    out_rows,
+    gathered,
+    spread,
+    factor_c,
+    factor_a,
+    factor_b,
+    send_a,
+    recv_a,
+    send_b,
+    recv_b,
+):
+    group = lax.axis_index("gx")
+    layer = lax.axis_index("gz")
+    me = group * 64 + layer
+    others = relative_devices(group, layer)
+    barrier = pltpu.get_barrier_semaphore()
+    for px, pz in others:
+        pl.semaphore_signal(barrier, inc=1, device_id=px * 64 + pz, device_id_type=LOGICAL)
+    pl.semaphore_wait(barrier, 255)
+    for px, pz in others:
+        peer = px * 64 + pz
+        pltpu.make_async_remote_copy(
+            src_ref=y_rows.at[pl.ds(peer, 1)],
+            dst_ref=gathered.at[group, pl.ds(layer, 1)],
+            send_sem=send_a,
+            recv_sem=recv_a,
+            device_id=peer,
+            device_id_type=LOGICAL,
+        ).start()
+    gathered[group, pl.ds(layer, 1)] = y_rows[pl.ds(me, 1)]
+    k_y = me.astype(jnp.float32) * (math.pi / 256)
+    k_x = lax.broadcasted_iota(jnp.int32, (1, 512), 1).astype(jnp.float32) * (math.pi / 512)
+    eigen = k_y * k_y + k_x * k_x
+    ratio = jnp.zeros((1, 512), jnp.float32)
+    for z in range(64):
+        lower = faces[0, z]
+        upper = faces[1, z]
+        per_metric = 2.0 / jnp.full((1, 512), lower + upper, jnp.float32)
+        inverse = 1.0 / (-(lower + upper) - eigen * per_metric - lower * ratio)
+        ratio = upper * inverse
+        factor_c[pl.ds(z, 1)] = ratio
+        factor_a[pl.ds(z, 1)] = lower * inverse
+        factor_b[pl.ds(z, 1)] = per_metric * inverse
+    rows = y_rows.at[pl.ds(0, 255)]
+    pltpu.make_async_copy(rows, rows, recv_a).wait()
+    coeffs = jnp.zeros((64, 512), jnp.float32)
+    for part in range(4):
+        coeffs = coeffs + lax.dot_general(
+            gathered[part],
+            x_cosines[:, part * 128 : part * 128 + 128],
+            (((1,), (1,)), ((), ())),
+            precision=lax.Precision.HIGHEST,
+            preferred_element_type=jnp.float32,
+        )
+    factor_b[...] = factor_b[...] * coeffs
+    value = jnp.zeros((1, 512), jnp.float32)
+    for z in range(64):
+        value = factor_b[pl.ds(z, 1)] - factor_a[pl.ds(z, 1)] * value
+        factor_b[pl.ds(z, 1)] = value
+    value = jnp.zeros((1, 512), jnp.float32)
+    for z in reversed(range(64)):
+        value = factor_b[pl.ds(z, 1)] - factor_c[pl.ds(z, 1)] * value
+        factor_b[pl.ds(z, 1)] = value
+    solved = factor_b[...]
+    for part in range(4):
+        spread[part] = jnp.dot(
+            solved,
+            x_cosines[:, part * 128 : part * 128 + 128],
+            precision=lax.Precision.HIGHEST,
+            preferred_element_type=jnp.float32,
+        )
+    for px, pz in others:
+        pltpu.make_async_remote_copy(
+            src_ref=spread.at[px, pl.ds(pz, 1)],
+            dst_ref=out_rows.at[pl.ds(me, 1)],
+            send_sem=send_b,
+            recv_sem=recv_b,
+            device_id=px * 64 + pz,
+            device_id_type=LOGICAL,
+        ).start()
+    out_rows[pl.ds(me, 1)] = spread[group, pl.ds(layer, 1)]
+    pltpu.make_async_copy(rows, rows, send_a).wait()
+    pltpu.make_async_copy(rows, rows, send_b).wait()
+    pltpu.make_async_copy(rows, rows, recv_b).wait()
+
+
+def spectral(face_metric, y_rows, x_cosines):
+    vmem = pl.BlockSpec(memory_space=pltpu.VMEM)
+    return pl.pallas_call(
+        spectral_kernel,
+        out_shape=jax.ShapeDtypeStruct((256, 128), jnp.float32),
+        in_specs=[pl.BlockSpec(memory_space=pltpu.SMEM), vmem, vmem],
+        out_specs=vmem,
+        scratch_shapes=[
+            pltpu.VMEM((4, 64, 128), jnp.float32),
+            pltpu.VMEM((4, 64, 128), jnp.float32),
+            pltpu.VMEM((64, 512), jnp.float32),
+            pltpu.VMEM((64, 512), jnp.float32),
+            pltpu.VMEM((64, 512), jnp.float32),
+            pltpu.SemaphoreType.DMA,
+            pltpu.SemaphoreType.DMA,
+            pltpu.SemaphoreType.DMA,
+            pltpu.SemaphoreType.DMA,
+        ],
+        compiler_params=pltpu.CompilerParams(collective_id=0, has_side_effects=True),
+    )(face_metric, y_rows, x_cosines)
 
 
 def per_device(velocity, earlier_term, face_metric):
@@ -109,9 +197,7 @@
     height = velocity.shape[2]
     breadth = velocity.shape[3]
     groups = lax.axis_size("gx")
-    layers_all = lax.axis_size("gz")
     length = breadth * groups
-    y_band = height // groups
     layer_index = lax.axis_index("gz")
     own_faces = lax.dynamic_slice_in_dim(face_metric, layer_index * z_cells, z_cells, 1)
     lower_face = own_faces[0][:, None, None]
@@ -151,31 +237,8 @@
     )
     source = divergence / TIME_STEP
     y_coeffs = transform_y(y_cosines, source)
-    grouped = lax.all_to_all(y_coeffs, "gx", split_axis=1, concat_axis=2, tiled=True)
-    x_cosines = cosine_table(length)
-    coeffs = lax.dot_general(
-        grouped.reshape(-1, length),
-        x_cosines,
-        (((1,), (1,)), ((), ())),
-        precision=lax.Precision.HIGHEST,
-    ).reshape(z_cells, y_band * length)
-    band_squares = lax.dynamic_slice_in_dim(y_squares, lax.axis_index("gx") * y_band, y_band, 0)
-    eigen_sum = (band_squares[:, None] + wave_squares(length)[None, :]).reshape(-1)
-    modes_local = y_band * length // layers_all
-    columns = lax.all_to_all(coeffs, "gz", split_axis=1, concat_axis=0, tiled=True)
-    eigen_local = lax.dynamic_slice_in_dim(eigen_sum, layer_index * modes_local, modes_local, 0)
-    whole_solved = solve_whole(
-        columns, eigen_local, face_metric[0][:, None], face_metric[1][:, None]
-    )
-    solved = lax.all_to_all(whole_solved, "gz", split_axis=0, concat_axis=1, tiled=True)
-    physical_x = lax.dot_general(
-        solved.reshape(-1, length),
-        x_cosines,
-        (((1,), (0,)), ((), ())),
-        precision=lax.Precision.HIGHEST,
-    ).reshape(z_cells, y_band, length)
-    spread = lax.all_to_all(physical_x, "gx", split_axis=2, concat_axis=1, tiled=True)
-    pressure = inverse_y(y_cosines, spread)
+    spread = spectral(face_metric, y_coeffs[0], cosine_table(length))
+    pressure = inverse_y(y_cosines, spread[None])
     wide_p = padded(pressure, (("gx", 2),), 1, True)
     press_x = 0.5 * (wide_p[..., 2:] - wide_p[..., :-2])
     wall_p = padded(pressure, (("gz", 0),), 1, False)

time: 125 us -> 89 us (0.71)
  Pallas kernels: 0 us -> 34.9 us
  blocking collectives: 22.1 us -> 0 us
  starting transfers between devices: 44.3 us -> 24.4 us
  waiting for transfers between devices: 21.2 us -> 6.04 us
  local copies, waits for them, and re-layouts: 15.6 us -> 9 us
  other arithmetic: 9.72 us -> 5.72 us
  matrix products: 8.15 us -> 6.51 us
    pallas_call x0 -> x1, Pallas kernels: none -> 34.9 us  [spectral(): pl.pallas_call(spectral_kernel, out_shape=jax.ShapeDtypeStruct((256, 128)...]
    all_to_all x2 -> x0, blocking collectives: 22.1 us -> none  [the longest x1 14.9 us: per_device(): lax.all_to_all(whole_solved, 'gz', split_axis=0, concat_axis=1, tiled=True)]
    all_to_all x2 -> x0, starting transfers between devices: 19.9 us -> none  [the longest x1 16.5 us: per_device(): lax.all_to_all(coeffs, 'gz', split_axis=1, concat_axis=0, tiled=True)]
    all_to_all x2 -> x0, waiting for transfers between devices: 15.5 us -> none  [the longest x1 10.9 us: per_device(): lax.all_to_all(coeffs, 'gz', split_axis=1, concat_axis=0, tiled=True)]
    dot_general x2 -> x0, matrix products: 2.92 us -> none  [the longest x1 1.8 us: per_device(): lax.dot_general(solved.reshape(-1, length), x_cosines, (((1,), (0,)), (()...]
    slice x117 -> x0, local copies, waits for them, and re-layouts: 2.59 us -> none  [the longest x83 1.62 us: solve_whole(): forward = lax.associative_scan(compose_rows, elements, axis=0)]
    unnamed x2 -> x0, other arithmetic: 2.01 us -> none
    unnamed x18 -> x14, local copies, waits for them, and re-layouts: 4.93 us -> 3.95 us
  transfers between devices with their start and end apart: 14 -> 12, of which waited for: 6 -> 4; matrix products, arithmetic and copies ran while one was open for 11% -> 15% of each run, Pallas kernels for 0% -> 0%
where the time goes in v1:
time: 89 us; the launch traced here: 88.6 us
  Pallas kernels  34.9 us (39%)
  starting transfers between devices  24.4 us (27%)
  local copies, waits for them, and re-layouts  9 us (10%)
  matrix products  6.51 us (7%)
  waiting for transfers between devices  6.04 us (7%)
  other arithmetic  5.72 us (6%)
  between operations  2.05 us (2%)
    pallas_call x1, Pallas kernels, spectral(): pl.pallas_call(spectral_kernel, out_shape=jax.ShapeDtypeStruct((256, 128)...  34.9 us
    ppermute x6, starting transfers between devices, padded(): lax.ppermute(head, axis, [((i + 1) % count, i) for i in range(ends)])  16.9 us
    ppermute x6, starting transfers between devices, padded(): lax.ppermute(tail, axis, [(i, (i + 1) % count) for i in range(ends)])  7.52 us
    ppermute x6, waiting for transfers between devices, padded(): lax.ppermute(tail, axis, [(i, (i + 1) % count) for i in range(ends)])  5.08 us
    mul x2, other arithmetic, cosine_table(): jnp.cos(residue.astype(jnp.float32) * (math.pi / (2 * extent)))  4.79 us
    dot_general x2, matrix products, inverse_y(): jnp.einsum('jy,zjx->zyx', cosines, field, precision=lax.Precision.HIGHEST)  4.58 us
    unnamed x14, local copies, waits for them, and re-layouts  3.95 us
    dot_general x2, matrix products, transform_y(): jnp.einsum('jy,zyx->zjx', cosines, field, precision=lax.Precision.HIGHEST)  1.93 us
  transfers between devices with their start and end apart: 12, of which 4 were waited for; matrix products, arithmetic and copies ran while one was open for 15% of the time, Pallas kernels for 0%

profile of v1, /device:TPU:1, one launch (start us, length us, event | category | flops | bytes accessed | tf_op | source)
XLA Modules:
  0.0 88.6 jit_solution(14401475351090856306)
XLA Ops:
  0.6 0.0 copy-start.1
  0.6 1.2 %copy.22 = f32[3,1,256,128]{2,3,0,1:T(8,128)S(1)} copy(f32[3,1,256,128]{3,2,1,0:T(8,128)} %param.7) | data formatting | bytes 786432 | tf_op args[0]
  1.9 5.1 %collective-permute-start.2 = (f32[3,1,256,128]{2,3,0,1:T(8,128)S(1)}, f32[3,1,256,128]{2,3,0,1:T(8,128)}, u32[]{:S(2)}, u32[]{:S(2)}) collective-permute-start(f32[3,1,256,128]{2,3,0,1:T(8,128)S(1)} %copy.22), channel_id=1, source_target_pairs={{1,0},{2,1},{3,2},{4,3},{5,4},{6,5},{7,6},{8,7},{9,8},{10,9},{11,1... | collective-permute-start | bytes 1179656 | tf_op jit(solution)/shard_map/ppermute | solution.py:26
  7.0 1.9 %collective-permute-start.3 = (f32[3,1,256,128]{2,3,0,1:T(8,128)S(1)}, f32[3,1,256,128]{2,3,0,1:T(8,128)}, u32[]{:S(2)}, u32[]{:S(2)}) collective-permute-start(f32[3,1,256,128]{2,3,0,1:T(8,128)S(1)} %copy.22), channel_id=1, source_target_pairs={{0,1},{1,2},{2,3},{3,4},{4,5},{5,6},{6,7},{7,8},{8,9},{9,10},{10,1... | collective-permute-start | bytes 1179656 | tf_op jit(solution)/shard_map/ppermute | solution.py:24
  8.9 0.6 fusion.58
  9.5 2.0 %collective-permute-start = (f32[3,1,256,1]{2,3,0,1:T(1,128)}, f32[3,1,256,1]{2,3,0,1:T(1,128)}, u32[]{:S(2)}, u32[]{:S(2)}) collective-permute-start(f32[3,1,256,1]{2,3,0,1:T(1,128)} %get-tuple-element.35), channel_id=1, source_target_pairs={{64,0},{128,64},{192,128},{0,192},{65,1},{129,65},{193,129},{1,193... | collective-permute-start | bytes 9224 | tf_op jit(solution)/shard_map/ppermute | solution.py:26
  11.5 0.0 collective-permute-start.1
  11.5 0.0 copy-done.1
  11.5 0.7 multiply_bitcast_fusion.2
  12.2 1.0 %fusion.23 = f32[256,256]{1,0:T(8,128)S(1)} fusion(s32[256]{0:T(256)S(1)} %multiply_add_fusion.1), kind=kLoop, calls=%fused_computation.37 | loop fusion | flops 983040 | bytes 263168 | tf_op jit(solution)/shard_map/mul | solution.py:37
  13.2 3.8 %fusion.5 = f32[512,512]{1,0:T(8,128)S(1)} fusion(s32[512]{0:T(512)S(1)} %multiply_add_fusion), kind=kLoop, calls=%fused_computation.12 | loop fusion | flops 3932160 | bytes 1050624 | tf_op jit(solution)/shard_map/mul | solution.py:37
  17.1 0.0 copy-start.4
  17.1 0.8 fusion
  17.9 0.0 copy-done.4
  17.9 0.1 constant_dynamic-slice_fusion
  18.0 0.0 copy-start.2
  18.0 0.2 fusion.60
  18.1 0.5 fusion.67
  18.7 0.2 copy-done.2
  18.9 0.8 copy.14
  19.6 0.8 copy.15
  20.4 0.7 copy.9
  21.1 0.0 copy-start.3
  21.1 0.1 copy.11
  21.3 0.8 copy.13
  22.1 0.0 copy-done.3
  22.1 0.8 copy.18
  23.0 0.0 copy-start
  24.1 0.0 collective-permute-done
  24.1 0.0 collective-permute-done.1
  24.1 0.0 collective-permute-done.2
  24.1 0.0 collective-permute-done.3
  24.1 3.3 %fusion.16 = f32[3,1,256,128]{2,3,0,1:T(8,128)S(1)} fusion(f32[3,1,256,128]{2,3,0,1:T(8,128)S(1)} %copy.22, f32[3,1,1,128]{2,3,0,1:T(8,128)S(1)} %copy.11, f32[3,1,255,128]{2,3,0,1:T(8,128)S(1)} %get-tuple-element.39, f32[3,1,255,128]{2,3,0,1:T(8,128)S(1)} %get-tuple-element.38, f32[3,1,1,128]{2,3,0,1:T(8,128)} %copy.13, ...), kind=kOutput, calls=%fused_computation.26 | convolution fusion | flops 305135616 | bytes 3610640 | tf_op jit(solution)/shard_map/jy,zjx->zyx/dot_general | solution.py:52
  27.4 0.0 copy-done
  27.5 3.2 %collective-permute-start.6 = (f32[1,256,128]{1,2,0:T(8,128)S(1)}, f32[1,256,128]{1,2,0:T(8,128)S(1)}, u32[]{:S(2)}, u32[]{:S(2)}) collective-permute-start(f32[1,256,128]{1,2,0:T(8,128)S(1)} %get-tuple-element.28), channel_id=1, source_target_pairs={{1,0},{2,1},{3,2},{4,3},{5,4},{6,5},{7,6},{8,7},{9,8},{10,9},{11,1... | collective-permute-start | bytes 393224 | tf_op jit(solution)/shard_map/ppermute | solution.py:26
  30.7 2.4 %collective-permute-start.7 = (f32[1,256,128]{1,2,0:T(8,128)S(1)}, f32[1,256,128]{1,2,0:T(8,128)S(1)}, u32[]{:S(2)}, u32[]{:S(2)}) collective-permute-start(f32[1,256,128]{1,2,0:T(8,128)S(1)} %get-tuple-element.28), channel_id=1, source_target_pairs={{0,1},{1,2},{2,3},{3,4},{4,5},{5,6},{6,7},{7,8},{8,9},{9,10},{10,1... | collective-permute-start | bytes 393224 | tf_op jit(solution)/shard_map/ppermute | solution.py:24
  33.1 0.1 fusion.65
  33.2 2.8 %collective-permute-start.4 = (f32[1,256,1]{1,2,0:T(1,128)S(1)}, f32[1,256,1]{1,2,0:T(1,128)S(1)}, u32[]{:S(2)}, u32[]{:S(2)}) collective-permute-start(f32[1,256,1]{1,2,0:T(1,128)S(1)} %get-tuple-element.50), channel_id=1, source_target_pairs={{64,0},{128,64},{192,128},{0,192},{65,1},{129,65},{193,129},{1,193... | collective-permute-start | bytes 3080 | tf_op jit(solution)/shard_map/ppermute | solution.py:26
  35.9 0.0 collective-permute-start.5
  35.9 0.1 fusion.64
  36.0 0.6 collective-permute-done.4
  36.6 2.9 %collective-permute-done.5 = f32[1,256,1]{1,2,0:T(1,128)S(1)} collective-permute-done((f32[1,256,1]{1,2,0:T(1,128)S(1)}, f32[1,256,1]{1,2,0:T(1,128)S(1)}, u32[]{:S(2)}, u32[]{:S(2)}) %collective-permute-start.5) | collective-permute-done | bytes 1056 | tf_op jit(solution)/shard_map/ppermute | solution.py:24
  39.6 0.0 collective-permute-done.6
  39.6 0.0 collective-permute-done.7
  39.6 1.1 %convolution_bitcast_fusion.2.y_rows = f32[256,128]{1,0:T(8,128)} fusion(f32[256,256]{1,0:T(8,128)S(1)} %scatter-mul.6, f32[1,256,128]{1,2,0:T(8,128)S(1)} %get-tuple-element.30, f32[1,256,1]{1,2,0:T(1,128)S(1)} %collective-permute-done.5, f32[1,256,1]{1,2,0:T(1,128)S(1)} %collective-permute-done.4, f32[1,1,128]{1,2,0:T(8,128)S(1)} %get-tuple-element.47, ...), kind=kOutput, calls=%fused_computation.7 | convolution fusion | flops 101056512 | bytes 1050628 | tf_op jit(solution)/shard_map/jy,zyx->zjx/dot_general | solution.py:48
  40.7 34.9 %shard_map.50 = f32[256,128]{1,0:T(8,128)} custom-call(f32[2,64]{1,0:T(2,128)} %faces.1, f32[256,128]{1,0:T(8,128)} %convolution_bitcast_fusion.2.y_rows, f32[512,512]{1,0:T(8,128)} %copy-done), custom_call_target="tpu_custom_call" | custom-call | tf_op jit(solution)/shard_map/pallas_call | solution.py:175
  75.6 1.3 %convolution_bitcast_fusion.1 = f32[1,256,128]{1,2,0:T(8,128)S(1)} fusion(f32[256,128]{1,0:T(8,128)} %shard_map.50, f32[256,256]{1,0:T(8,128)S(1)} %scatter-mul.6), kind=kOutput, calls=%fused_computation.6 | convolution fusion | flops 100663296 | bytes 524288 | tf_op jit(solution)/shard_map/jy,zjx->zyx/dot_general | solution.py:52
  76.9 0.1 fusion.63
  77.0 0.1 fusion.62
  77.1 2.6 %collective-permute-start.10 = (f32[1,256,128]{1,2,0:T(8,128)S(1)}, f32[1,256,128]{1,2,0:T(8,128)S(1)}, u32[]{:S(2)}, u32[]{:S(2)}) collective-permute-start(f32[1,256,128]{1,2,0:T(8,128)S(1)} %convolution_bitcast_fusion.1), channel_id=1, source_target_pairs={{1,0},{2,1},{3,2},{4,3},{5,4},{6,5},{7,6},{8,7},{9,8},{10,9},{11,1... | collective-permute-start | bytes 393224 | tf_op jit(solution)/shard_map/ppermute | solution.py:26
  79.7 2.9 %collective-permute-start.11 = (f32[1,256,128]{1,2,0:T(8,128)S(1)}, f32[1,256,128]{1,2,0:T(8,128)S(1)}, u32[]{:S(2)}, u32[]{:S(2)}) collective-permute-start(f32[1,256,128]{1,2,0:T(8,128)S(1)} %convolution_bitcast_fusion.1), channel_id=1, source_target_pairs={{0,1},{1,2},{2,3},{3,4},{4,5},{5,6},{6,7},{7,8},{8,9},{9,10},{10,1... | collective-permute-start | bytes 393224 | tf_op jit(solution)/shard_map/ppermute | solution.py:24
  82.7 1.3 %collective-permute-start.8 = (f32[1,256,1]{1,2,0:T(1,128)S(1)}, f32[1,256,1]{1,2,0:T(1,128)S(1)}, u32[]{:S(2)}, u32[]{:S(2)}) collective-permute-start(f32[1,256,1]{1,2,0:T(1,128)S(1)} %get-tuple-element.40), channel_id=1, source_target_pairs={{64,0},{128,64},{192,128},{0,192},{65,1},{129,65},{193,129},{1,193... | collective-permute-start | bytes 3080 | tf_op jit(solution)/shard_map/ppermute | solution.py:26
  83.9 0.3 collective-permute-start.9
  84.2 0.1 fusion.49
  84.3 0.8 copy.30
  85.1 0.3 collective-permute-done.8
  85.4 2.2 %collective-permute-done.9 = f32[1,256,1]{1,2,0:T(1,128)S(1)} collective-permute-done((f32[1,256,1]{1,2,0:T(1,128)S(1)}, f32[1,256,1]{1,2,0:T(1,128)S(1)}, u32[]{:S(2)}, u32[]{:S(2)}) %collective-permute-start.9) | collective-permute-done | bytes 1056 | tf_op jit(solution)/shard_map/ppermute | solution.py:24
  87.6 0.0 collective-permute-done.10
  87.6 0.0 collective-permute-done.11
  87.7 0.1 fusion.17
  87.7 0.9 %copy.29 = f32[3,1,256,128]{3,2,1,0:T(8,128)} copy(f32[3,1,256,128]{2,3,0,1:T(8,128)S(1)} %fusion.17) | data formatting | bytes 786432
  (13 shorter events, 0.2 us)
Async XLA Ops:
  0.6 10.9 %copy-start.1 = (f32[3,1,256,128]{3,2,1,0:T(8,128)S(1)}, f32[3,1,256,128]{3,2,1,0:T(8,128)}, u32[]{:S(2)}) copy-start(f32[3,1,256,128]{3,2,1,0:T(8,128)} %param.7) | copy-start | bytes 1179652
  1.9 22.3 %collective-permute-start.2 = (f32[3,1,256,128]{2,3,0,1:T(8,128)S(1)}, f32[3,1,256,128]{2,3,0,1:T(8,128)}, u32[]{:S(2)}, u32[]{:S(2)}) collective-permute-start(f32[3,1,256,128]{2,3,0,1:T(8,128)S(1)} %copy.22), channel_id=1, source_target_pairs={{1,0},{2,1},{3,2},{4,3},{5,4},{6,5},{7,6},{8,7},{9,8},{10,9},{11,1... | collective-permute-start | bytes 1179656 | tf_op jit(solution)/shard_map/ppermute | solution.py:26
  7.0 17.1 %collective-permute-start.3 = (f32[3,1,256,128]{2,3,0,1:T(8,128)S(1)}, f32[3,1,256,128]{2,3,0,1:T(8,128)}, u32[]{:S(2)}, u32[]{:S(2)}) collective-permute-start(f32[3,1,256,128]{2,3,0,1:T(8,128)S(1)} %copy.22), channel_id=1, source_target_pairs={{0,1},{1,2},{2,3},{3,4},{4,5},{5,6},{6,7},{7,8},{8,9},{9,10},{10,1... | collective-permute-start | bytes 1179656 | tf_op jit(solution)/shard_map/ppermute | solution.py:24
  9.5 14.6 %collective-permute-start = (f32[3,1,256,1]{2,3,0,1:T(1,128)}, f32[3,1,256,1]{2,3,0,1:T(1,128)}, u32[]{:S(2)}, u32[]{:S(2)}) collective-permute-start(f32[3,1,256,1]{2,3,0,1:T(1,128)} %get-tuple-element.35), channel_id=1, source_target_pairs={{64,0},{128,64},{192,128},{0,192},{65,1},{129,65},{193,129},{1,193... | collective-permute-start | bytes 9224 | tf_op jit(solution)/shard_map/ppermute | solution.py:26
  11.5 12.6 %collective-permute-start.1 = (f32[3,1,256,1]{2,3,0,1:T(1,128)}, f32[3,1,256,1]{2,3,0,1:T(1,128)}, u32[]{:S(2)}, u32[]{:S(2)}) collective-permute-start(f32[3,1,256,1]{2,3,0,1:T(1,128)} %get-tuple-element.34), channel_id=1, source_target_pairs={{0,64},{64,128},{128,192},{192,0},{1,65},{65,129},{129,193},{193,1... | collective-permute-start | bytes 9224 | tf_op jit(solution)/shard_map/ppermute | solution.py:24
  17.1 0.8 copy-start.4
  18.0 0.9 %copy-start.2 = (f32[256,128]{1,0:T(8,128)S(1)}, f32[256,128]{1,0:T(8,128)}, u32[]{:S(2)}) copy-start(f32[256,128]{1,0:T(8,128)} %get-tuple-element.33) | copy-start | bytes 393220
  21.1 1.0 %copy-start.3 = (bf16[3,1,256,128]{3,2,1,0:T(8,128)(2,1)S(1)}, bf16[3,1,256,128]{3,2,1,0:T(8,128)(2,1)}, u32[]{:S(2)}) copy-start(bf16[3,1,256,128]{3,2,1,0:T(8,128)(2,1)} %param.8) | copy-start | bytes 589828
  23.0 4.5 %copy-start = (f32[512,512]{1,0:T(8,128)}, f32[512,512]{1,0:T(8,128)S(1)}, u32[]{:S(2)}) copy-start(f32[512,512]{1,0:T(8,128)S(1)} %scatter-mul.9.x_cosines) | copy-start | bytes 3145732
  27.5 12.1 %collective-permute-start.6 = (f32[1,256,128]{1,2,0:T(8,128)S(1)}, f32[1,256,128]{1,2,0:T(8,128)S(1)}, u32[]{:S(2)}, u32[]{:S(2)}) collective-permute-start(f32[1,256,128]{1,2,0:T(8,128)S(1)} %get-tuple-element.28), channel_id=1, source_target_pairs={{1,0},{2,1},{3,2},{4,3},{5,4},{6,5},{7,6},{8,7},{9,8},{10,9},{11,1... | collective-permute-start | bytes 393224 | tf_op jit(solution)/shard_map/ppermute | solution.py:26
  30.7 8.9 %collective-permute-start.7 = (f32[1,256,128]{1,2,0:T(8,128)S(1)}, f32[1,256,128]{1,2,0:T(8,128)S(1)}, u32[]{:S(2)}, u32[]{:S(2)}) collective-permute-start(f32[1,256,128]{1,2,0:T(8,128)S(1)} %get-tuple-element.28), channel_id=1, source_target_pairs={{0,1},{1,2},{2,3},{3,4},{4,5},{5,6},{6,7},{7,8},{8,9},{9,10},{10,1... | collective-permute-start | bytes 393224 | tf_op jit(solution)/shard_map/ppermute | solution.py:24
  33.2 3.5 %collective-permute-start.4 = (f32[1,256,1]{1,2,0:T(1,128)S(1)}, f32[1,256,1]{1,2,0:T(1,128)S(1)}, u32[]{:S(2)}, u32[]{:S(2)}) collective-permute-start(f32[1,256,1]{1,2,0:T(1,128)S(1)} %get-tuple-element.50), channel_id=1, source_target_pairs={{64,0},{128,64},{192,128},{0,192},{65,1},{129,65},{193,129},{1,193... | collective-permute-start | bytes 3080 | tf_op jit(solution)/shard_map/ppermute | solution.py:26
  35.9 3.6 %collective-permute-start.5 = (f32[1,256,1]{1,2,0:T(1,128)S(1)}, f32[1,256,1]{1,2,0:T(1,128)S(1)}, u32[]{:S(2)}, u32[]{:S(2)}) collective-permute-start(f32[1,256,1]{1,2,0:T(1,128)S(1)} %get-tuple-element.51), channel_id=1, source_target_pairs={{0,64},{64,128},{128,192},{192,0},{1,65},{65,129},{129,193},{193,1... | collective-permute-start | bytes 3080 | tf_op jit(solution)/shard_map/ppermute | solution.py:24
  77.1 10.5 %collective-permute-start.10 = (f32[1,256,128]{1,2,0:T(8,128)S(1)}, f32[1,256,128]{1,2,0:T(8,128)S(1)}, u32[]{:S(2)}, u32[]{:S(2)}) collective-permute-start(f32[1,256,128]{1,2,0:T(8,128)S(1)} %convolution_bitcast_fusion.1), channel_id=1, source_target_pairs={{1,0},{2,1},{3,2},{4,3},{5,4},{6,5},{7,6},{8,7},{9,8},{10,9},{11,1... | collective-permute-start | bytes 393224 | tf_op jit(solution)/shard_map/ppermute | solution.py:26
  79.7 7.9 %collective-permute-start.11 = (f32[1,256,128]{1,2,0:T(8,128)S(1)}, f32[1,256,128]{1,2,0:T(8,128)S(1)}, u32[]{:S(2)}, u32[]{:S(2)}) collective-permute-start(f32[1,256,128]{1,2,0:T(8,128)S(1)} %convolution_bitcast_fusion.1), channel_id=1, source_target_pairs={{0,1},{1,2},{2,3},{3,4},{4,5},{5,6},{6,7},{7,8},{8,9},{9,10},{10,1... | collective-permute-start | bytes 393224 | tf_op jit(solution)/shard_map/ppermute | solution.py:24
  82.7 2.7 %collective-permute-start.8 = (f32[1,256,1]{1,2,0:T(1,128)S(1)}, f32[1,256,1]{1,2,0:T(1,128)S(1)}, u32[]{:S(2)}, u32[]{:S(2)}) collective-permute-start(f32[1,256,1]{1,2,0:T(1,128)S(1)} %get-tuple-element.40), channel_id=1, source_target_pairs={{64,0},{128,64},{192,128},{0,192},{65,1},{129,65},{193,129},{1,193... | collective-permute-start | bytes 3080 | tf_op jit(solution)/shard_map/ppermute | solution.py:26
  83.9 3.6 %collective-permute-start.9 = (f32[1,256,1]{1,2,0:T(1,128)S(1)}, f32[1,256,1]{1,2,0:T(1,128)S(1)}, u32[]{:S(2)}, u32[]{:S(2)}) collective-permute-start(f32[1,256,1]{1,2,0:T(1,128)S(1)} %get-tuple-element.41), channel_id=1, source_target_pairs={{0,64},{64,128},{128,192},{192,0},{1,65},{65,129},{129,193},{193,1... | collective-permute-start | bytes 3080 | tf_op jit(solution)/shard_map/ppermute | solution.py:24

commit v2 on v0

v2 whole, which is shorter than its diff:
```python
import math

import jax
import jax.numpy as jnp
import numpy as np
from jax import lax
from jax.experimental import pallas as pl
from jax.experimental.pallas import tpu as pltpu
from jax.sharding import PartitionSpec as P

TIME_STEP = 0.4
ADVECT_WEIGHT = 5.0 / 12.0
EARLIER_WEIGHT = -17.0 / 60.0
VISCOUS_WEIGHT = 2.0 / 15.0
NX = 512
NY = 256
NZ = 64
LANES = 128
PEERS = 256
LOGICAL = pl.DeviceIdType.LOGICAL
F32 = jnp.float32
BF16 = jnp.bfloat16
NN = (((1,), (0,)), ((), ()))
NT = (((1,), (1,)), ((), ()))
TN = (((0,), (0,)), ((), ()))
Y_SHIFTS = [(i, k, m) for k in (2, 1, 3, 0) for i in (2, 1, 3, 0) for m in (1, 0)]


def cosine_table(extent):
    wavenumber = np.arange(extent)[:, None]
    points = np.arange(extent)[None, :]
    residue = wavenumber * (2 * points + 1) % (4 * extent)
    cosines = np.cos(residue * (math.pi / (2 * extent))) * math.sqrt(2.0 / extent)
    cosines[0] *= math.sqrt(0.5)
    return cosines


def halves(table):
    high = table.astype(np.float32).astype(jnp.bfloat16)
    low = (table - high.astype(np.float64)).astype(np.float32).astype(jnp.bfloat16)
    return np.stack([high, low])


def split(values):
    high = values.astype(BF16)
    low = (values - high.astype(F32)).astype(BF16)
    return high, low


def mul(a, b, dims):
    return lax.dot_general(a, b, dims, preferred_element_type=F32)


def table_times(table, values):
    high, low = split(values)
    t_high, t_low = table[0], table[1]
    return mul(t_high, high, NN) + (mul(t_high, low, NN) + mul(t_low, high, NN))


def times_table(values, table, dims):
    high, low = split(values)
    t_high, t_low = table[0], table[1]
    return mul(high, t_high, dims) + (mul(high, t_low, dims) + mul(low, t_high, dims))


def row_ids(shape):
    return lax.broadcasted_iota(jnp.int32, shape, 0)


def lane_ids(shape):
    return lax.broadcasted_iota(jnp.int32, shape, 1)


def y_neighbours(field):
    rows = row_ids(field.shape)
    count = field.shape[0]
    after = jnp.where(rows == count - 1, field, pltpu.roll(field, count - 1, 0))
    before = jnp.where(rows == 0, field, pltpu.roll(field, 1, 0))
    return after, before


def z_slope(columns, metric):
    rows = row_ids(columns.shape)
    count = columns.shape[0]
    after = jnp.where(rows == count - 1, 0.0, pltpu.roll(columns, count - 1, 0))
    before = jnp.where(rows == 0, 0.0, pltpu.roll(columns, 1, 0))
    return metric * (0.5 * (after - before))


def x_slope(lines):
    count = lines.shape[1]
    return 0.5 * (pltpu.roll(lines, count - 1, 1) - pltpu.roll(lines, 1, 1))


def step_kernel(
    faces,
    velocity,
    earlier,
    y_second,
    y_forward,
    y_inverse,
    x_table,
    new_velocity,
    pressure,
    edges,
    edges_in,
    below,
    above,
    partial,
    y_rows,
    gathered,
    metrics,
    factor_c,
    factor_a,
    factor_b,
    spread,
    returned,
    edge_send,
    edge_recv,
    halo_send,
    halo_recv,
    out_send,
    out_recv,
    back_send,
    back_recv,
):
    group = lax.axis_index("gx")
    layer = lax.axis_index("gz")
    me = group * 64 + layer
    y_parts = [((layer & 6) + (shift << 1)) & 6 for shift in range(4)]
    core_parts = [layer & 1, (layer & 1) ^ 1]
    x_parts = [(group + shift) & 3 for shift in range(4)]

    def each_peer(act):
        def at_shift(shift, combos):
            z_part = ((layer & 56) + (shift << 3)) & 56
            for i, k, m in combos:
                act(x_parts[i], z_part | (y_parts[k] | core_parts[m]))

        def body(j, carry):
            at_shift(4 + (1 - 2 * (j & 1)) * ((j + 1) >> 1), Y_SHIFTS)
            return carry

        lax.fori_loop(0, 7, body, 0)
        at_shift(0, [c for c in Y_SHIFTS if c != (0, 0, 0)])

    barrier = pltpu.get_barrier_semaphore()

    def greet(px, pz):
        pl.semaphore_signal(barrier, inc=1, device_id=px * 64 + pz, device_id_type=LOGICAL)

    each_peer(greet)

    pick_shape = (8, LANES)
    picks = (row_ids(pick_shape) == 0) & (lane_ids(pick_shape) == 0)
    picks |= (row_ids(pick_shape) == 1) & (lane_ids(pick_shape) == LANES - 1)
    picks = picks.astype(F32).astype(BF16)
    for c in range(3):
        high, low = split(velocity[c, 0])
        edges[:, c * NY : c * NY + NY] = mul(picks, high, NT) + mul(picks, low, NT)

    pl.semaphore_wait(barrier, PEERS - 1)

    x_right = ((group + 1) & 3) * 64 + layer
    x_left = ((group + 3) & 3) * 64 + layer
    z_up = group * 64 + ((layer + 1) & 63)
    z_down = group * 64 + ((layer + 63) & 63)

    def remote(source, target, send, recv, peer):
        return pltpu.make_async_remote_copy(
            src_ref=source,
            dst_ref=target,
            send_sem=send,
            recv_sem=recv,
            device_id=peer,
            device_id_type=LOGICAL,
        )

    to_right = remote(edges, edges_in.at[0], edge_send.at[0], edge_recv.at[0], x_right)
    to_left = remote(edges, edges_in.at[1], edge_send.at[1], edge_recv.at[1], x_left)
    to_right.start()
    to_left.start()
    halos = {}
    for c in (0, 2, 1):
        up = remote(velocity.at[c, 0], below.at[c], halo_send.at[0, c], halo_recv.at[0, c], z_up)
        down = remote(velocity.at[c, 0], above.at[c], halo_send.at[1, c], halo_recv.at[1, c], z_down)
        up.start()
        down.start()
        halos[c] = (up, down)

    u = velocity[0, 0]
    v = velocity[1, 0]
    for c in (0, 2, 1):
        field = velocity[c, 0]
        after, before = y_neighbours(field)
        bend = table_times(y_second, field) - 2.0 * field
        partial[c] = field + TIME_STEP * (
            EARLIER_WEIGHT * earlier[c, 0].astype(F32)
            + VISCOUS_WEIGHT * bend
            - ADVECT_WEIGHT * (v * (0.5 * (after - before)))
        )

    k_y = me.astype(F32) * (math.pi / NY)
    k_x = lane_ids((1, NX)).astype(F32) * (math.pi / NX)
    eigen = k_y * k_y + k_x * k_x
    ratio = jnp.zeros((1, NX), F32)
    for z in range(NZ):
        lower = faces[0, z]
        upper = faces[1, z]
        metrics[pl.ds(z, 1)] = jnp.full((1, LANES), 0.5 * (lower + upper), F32)
        per_metric = 2.0 / jnp.full((1, NX), lower + upper, F32)
        inverse = 1.0 / (-(lower + upper) - eigen * per_metric - lower * ratio)
        ratio = upper * inverse
        factor_c[pl.ds(z, 1)] = ratio
        factor_a[pl.ds(z, 1)] = lower * inverse
        factor_b[pl.ds(z, 1)] = (per_metric * inverse) * (1.0 / TIME_STEP)

    to_right.wait()
    to_left.wait()
    place_shape = (16, LANES)
    places = (row_ids(place_shape) == 1) & (lane_ids(place_shape) == 0)
    places |= (row_ids(place_shape) == 8) & (lane_ids(place_shape) == LANES - 1)
    places = places.astype(F32).astype(BF16)
    lanes = lane_ids((NY, LANES))
    for c in (0, 2, 1):
        field = velocity[c, 0]
        part = slice(c * NY, c * NY + NY)
        high, low = split(jnp.concatenate([edges_in[0, :, part], edges_in[1, :, part]], 0))
        outer = mul(high, places, TN) + mul(low, places, TN)
        after = jnp.where(lanes == LANES - 1, outer, pltpu.roll(field, LANES - 1, 1))
        before = jnp.where(lanes == 0, outer, pltpu.roll(field, 1, 1))
        partial[c] = partial[c] + TIME_STEP * (
            VISCOUS_WEIGHT * (after + before) - ADVECT_WEIGHT * (u * (0.5 * (after - before)))
        )

    lower = faces[0, layer]
    upper = faces[1, layer]
    metric = 0.5 * (lower + upper)
    w = velocity[2, 0]
    for c in (0, 2, 1):
        for copy in halos[c]:
            copy.wait()
        field = velocity[c, 0]
        after = jnp.where(layer == NZ - 1, 0.0, above[c])
        before = jnp.where(layer == 0, 0.0, below[c])
        bend = metric * (upper * (after - field) - lower * (field - before))
        predicted = partial[c] + TIME_STEP * (
            VISCOUS_WEIGHT * bend - ADVECT_WEIGHT * (w * (metric * (0.5 * (after - before))))
        )
        partial[c] = predicted
        if c == 1:
            after, before = y_neighbours(predicted)
            predicted = 0.5 * (after - before)
        y_rows[c] = table_times(y_forward, predicted)

        def send(px, pz):
            peer = px * 64 + pz
            remote(
                y_rows.at[c, pl.ds(peer, 1)],
                gathered.at[c, group, pl.ds(layer, 1)],
                out_send.at[c],
                out_recv.at[c],
                peer,
            ).start()

        each_peer(send)
        gathered[c, group, pl.ds(layer, 1)] = y_rows[c, pl.ds(me, 1)]

    others = returned.at[0, pl.ds(0, PEERS - 1)]

    def finish(sem):
        pltpu.make_async_copy(others, others, sem).wait()

    def lines(c):
        return jnp.concatenate([gathered[c, part] for part in range(4)], 1)

    metric_rows = jnp.concatenate([metrics[...]] * 4, 1)
    finish(out_recv.at[0])
    source = x_slope(lines(0))
    finish(out_recv.at[2])
    source = source + z_slope(lines(2), metric_rows)
    finish(out_recv.at[1])
    source = source + lines(1)
    factor_b[...] = factor_b[...] * times_table(source, x_table, NT)
    value = jnp.zeros((1, NX), F32)
    for z in range(NZ):
        value = factor_b[pl.ds(z, 1)] - factor_a[pl.ds(z, 1)] * value
        factor_b[pl.ds(z, 1)] = value
    value = jnp.zeros((1, NX), F32)
    for z in reversed(range(NZ)):
        value = factor_b[pl.ds(z, 1)] - factor_c[pl.ds(z, 1)] * value
        factor_b[pl.ds(z, 1)] = value
    solved = times_table(factor_b[...], x_table, NN)
    for c, lined in ((1, solved), (0, x_slope(solved)), (2, z_slope(solved, metric_rows))):
        for part in range(4):
            spread[c, part] = lined[:, part * LANES : part * LANES + LANES]

        def send_back(px, pz):
            remote(
                spread.at[c, px, pl.ds(pz, 1)],
                returned.at[c, pl.ds(me, 1)],
                back_send.at[c],
                back_recv.at[c],
                px * 64 + pz,
            ).start()

        each_peer(send_back)
        returned[c, pl.ds(me, 1)] = spread[c, group, pl.ds(layer, 1)]

    for c in (1, 0, 2):
        finish(back_recv.at[c])
        field = table_times(y_inverse, returned[c])
        if c == 1:
            pressure[0] = field
            after, before = y_neighbours(field)
            field = 0.5 * (after - before)
        new_velocity[c, 0] = partial[c] - TIME_STEP * field
    for c in range(3):
        finish(out_send.at[c])
        finish(back_send.at[c])


def per_device(velocity, earlier_term, face_metric):
    y_cosines = cosine_table(NY)
    y_squares = (np.arange(NY) * (math.pi / NY)) ** 2
    y_second = -(y_cosines.T * y_squares) @ y_cosines
    vmem = pl.BlockSpec(memory_space=pltpu.VMEM)
    dma = pltpu.SemaphoreType.DMA
    return pl.pallas_call(
        step_kernel,
        out_shape=(
            jax.ShapeDtypeStruct(velocity.shape, F32),
            jax.ShapeDtypeStruct(velocity.shape[1:], F32),
        ),
        in_specs=[pl.BlockSpec(memory_space=pltpu.SMEM)] + [vmem] * 6,
        out_specs=(vmem, vmem),
        scratch_shapes=[
            pltpu.VMEM((8, 3 * NY), F32),
            pltpu.VMEM((2, 8, 3 * NY), F32),
            pltpu.VMEM((3, NY, LANES), F32),
            pltpu.VMEM((3, NY, LANES), F32),
            pltpu.VMEM((3, NY, LANES), F32),
            pltpu.VMEM((3, NY, LANES), F32),
            pltpu.VMEM((3, 4, NZ, LANES), F32),
            pltpu.VMEM((NZ, LANES), F32),
            pltpu.VMEM((NZ, NX), F32),
            pltpu.VMEM((NZ, NX), F32),
            pltpu.VMEM((NZ, NX), F32),
            pltpu.VMEM((3, 4, NZ, LANES), F32),
            pltpu.VMEM((3, NY, LANES), F32),
            dma((2,)),
            dma((2,)),
            dma((2, 3)),
            dma((2, 3)),
            dma((3,)),
            dma((3,)),
            dma((3,)),
            dma((3,)),
        ],
        compiler_params=pltpu.CompilerParams(collective_id=0, has_side_effects=True),
    )(
        face_metric,
        velocity,
        earlier_term,
        jnp.asarray(halves(y_second)),
        jnp.asarray(halves(y_cosines)),
        jnp.asarray(halves(y_cosines.T)),
        jnp.asarray(halves(cosine_table(NX))),
    )


def solution(mesh):
    placed = (P(None, "gz", None, "gx"), P(None, "gz", None, "gx"), P())
    return jax.shard_map(
        per_device,
        mesh=mesh,
        in_specs=placed,
        out_specs=(P(None, "gz", None, "gx"), P("gz", None, "gx")),
        check_vma=False,
    )
```

time: 125 us -> 51.9 us (0.42)
  Pallas kernels: 0 us -> 48.6 us
  starting transfers between devices: 44.3 us -> 0 us
  blocking collectives: 22.1 us -> 0 us
  waiting for transfers between devices: 21.2 us -> 0 us
  local copies, waits for them, and re-layouts: 15.6 us -> 2.46 us
  other arithmetic: 9.72 us -> 0 us
  matrix products: 8.15 us -> 0 us
  between operations: 3.13 us -> 0.65 us
    pallas_call x0 -> x1, Pallas kernels: none -> 48.6 us  [per_device(): pl.pallas_call(step_kernel, out_shape=(jax.ShapeDtypeStruct(velocity.shap...]
    ppermute x12 -> x0, starting transfers between devices: 24.4 us -> none  [the longest x6 17.4 us: padded(): lax.ppermute(head, axis, [((i + 1) % count, i) for i in range(ends)])]
    all_to_all x2 -> x0, blocking collectives: 22.1 us -> none  [the longest x1 14.9 us: per_device(): lax.all_to_all(whole_solved, 'gz', split_axis=0, concat_axis=1, tiled=True)]
    all_to_all x2 -> x0, starting transfers between devices: 19.9 us -> none  [the longest x1 16.5 us: per_device(): lax.all_to_all(coeffs, 'gz', split_axis=1, concat_axis=0, tiled=True)]
    all_to_all x2 -> x0, waiting for transfers between devices: 15.5 us -> none  [the longest x1 10.9 us: per_device(): lax.all_to_all(coeffs, 'gz', split_axis=1, concat_axis=0, tiled=True)]
    dot_general x6 -> x0, matrix products: 8.15 us -> none  [the longest x2 4.21 us: inverse_y(): jnp.einsum('jy,zjx->zyx', cosines, field, precision=lax.Precision.HIGHEST)]
    mul x22 -> x0, other arithmetic: 5.89 us -> none  [the longest x2 4.79 us: cosine_table(): jnp.cos(residue.astype(jnp.float32) * (math.pi / (2 * extent)))]
    ppermute x12 -> x0, waiting for transfers between devices: 5.74 us -> none  [the longest x6 5.01 us: padded(): lax.ppermute(tail, axis, [(i, (i + 1) % count) for i in range(ends)])]
  transfers between devices with their start and end apart: 14 -> 0, of which waited for: 6 -> 0; matrix products, arithmetic and copies ran while one was open for 11% -> 0% of each run, Pallas kernels for 0% -> 0%
where the time goes in v2:
time: 51.9 us; the launch traced here: 51.8 us
  Pallas kernels  48.6 us (94%)
  local copies, waits for them, and re-layouts  2.46 us (5%)
  between operations  0.65 us (1%)
    pallas_call x1, Pallas kernels, per_device(): pl.pallas_call(step_kernel, out_shape=(jax.ShapeDtypeStruct(velocity.shap...  48.6 us
    unnamed x4, local copies, waits for them, and re-layouts  2.46 us

profile of v2, /device:TPU:1, one launch (start us, length us, event | category | flops | bytes accessed | tf_op | source)
XLA Modules:
  0.0 51.8 jit_solution(8605425552951051163)
XLA Ops:
  0.6 48.6 %shard_map.86 = (f32[3,1,256,128]{3,2,1,0:T(8,128)}, f32[1,256,128]{2,1,0:T(8,128)}) custom-call(f32[2,64]{1,0:T(2,128)} %faces.1, f32[3,1,256,128]{3,2,1,0:T(8,128)} %velocity.1, bf16[3,1,256,128]{3,2,1,0:T(8,128)(2,1)} %earlier.1, bf16[2,256,256]{2,1,0:T(8,128)(2,1)} %constant.8.clone.y_second, bf16[2,256,256]{2,1,0:T(8,128)(2,1)} %constant.9.clone.y_forward, ...), custom_call_target="tpu_custom_call" | custom-call | tf_op jit(solution)/shard_map/pallas_call | solution.py:329
  49.3 0.0 copy-start
  49.3 1.8 %copy.11 = f32[3,1,256,128]{3,2,1,0:T(8,128)} copy(f32[3,1,256,128]{3,2,1,0:T(8,128)} %get-tuple-element.4) | data formatting | bytes 786432
  51.1 0.0 copy-done
  51.1 0.7 %copy.12 = f32[1,256,128]{2,1,0:T(8,128)} copy(f32[1,256,128]{2,1,0:T(8,128)S(1)} %copy-done) | data formatting | bytes 262144
Async XLA Ops:
  49.3 1.8 %copy-start = (f32[1,256,128]{2,1,0:T(8,128)S(1)}, f32[1,256,128]{2,1,0:T(8,128)}, u32[]{:S(2)}) copy-start(f32[1,256,128]{2,1,0:T(8,128)} %get-tuple-element.5) | copy-start | bytes 393220

commit v3 on v2

v3 whole, which is shorter than its diff:
```python
import math

import jax
import jax.numpy as jnp
import numpy as np
from jax import lax
from jax.experimental import pallas as pl
from jax.experimental.pallas import tpu as pltpu
from jax.sharding import PartitionSpec as P

TIME_STEP = 0.4
ADVECT_WEIGHT = 5.0 / 12.0
EARLIER_WEIGHT = -17.0 / 60.0
VISCOUS_WEIGHT = 2.0 / 15.0
NX = 512
NY = 256
NZ = 64
LANES = 128
PEERS = 256
LOGICAL = pl.DeviceIdType.LOGICAL
F32 = jnp.float32
BF16 = jnp.bfloat16
NN = (((1,), (0,)), ((), ()))
NT = (((1,), (1,)), ((), ()))
TN = (((0,), (0,)), ((), ()))
Y_SHIFTS = [(i, k, m) for k in (2, 1, 3, 0) for i in (2, 1, 3, 0) for m in (1, 0)]


def cosine_table(extent):
    wavenumber = np.arange(extent)[:, None]
    points = np.arange(extent)[None, :]
    residue = wavenumber * (2 * points + 1) % (4 * extent)
    cosines = np.cos(residue * (math.pi / (2 * extent))) * math.sqrt(2.0 / extent)
    cosines[0] *= math.sqrt(0.5)
    return cosines


def halves(table):
    high = table.astype(np.float32).astype(jnp.bfloat16)
    low = (table - high.astype(np.float64)).astype(np.float32).astype(jnp.bfloat16)
    return np.stack([high, low])


def split(values):
    high = values.astype(BF16)
    low = (values - high.astype(F32)).astype(BF16)
    return high, low


def mul(a, b, dims):
    return lax.dot_general(a, b, dims, preferred_element_type=F32)


def table_times(table, values):
    high, low = split(values)
    t_high, t_low = table[0], table[1]
    return mul(t_high, high, NN) + (mul(t_high, low, NN) + mul(t_low, high, NN))


def times_table(values, table, dims):
    high, low = split(values)
    t_high, t_low = table[0], table[1]
    return mul(high, t_high, dims) + (mul(high, t_low, dims) + mul(low, t_high, dims))


def row_ids(shape):
    return lax.broadcasted_iota(jnp.int32, shape, 0)


def lane_ids(shape):
    return lax.broadcasted_iota(jnp.int32, shape, 1)


def y_neighbours(field):
    rows = row_ids(field.shape)
    count = field.shape[0]
    after = jnp.where(rows == count - 1, field, pltpu.roll(field, count - 1, 0))
    before = jnp.where(rows == 0, field, pltpu.roll(field, 1, 0))
    return after, before


def z_slope(columns, metric):
    rows = row_ids(columns.shape)
    count = columns.shape[0]
    after = jnp.where(rows == count - 1, 0.0, pltpu.roll(columns, count - 1, 0))
    before = jnp.where(rows == 0, 0.0, pltpu.roll(columns, 1, 0))
    return metric * (0.5 * (after - before))


def x_slope(lines):
    count = lines.shape[1]
    return 0.5 * (pltpu.roll(lines, count - 1, 1) - pltpu.roll(lines, 1, 1))


def lined_x(field, edge_rows):
    shape = (16, LANES)
    places = (row_ids(shape) == 1) & (lane_ids(shape) == 0)
    places |= (row_ids(shape) == 8) & (lane_ids(shape) == LANES - 1)
    places = places.astype(F32).astype(BF16)
    high, low = split(edge_rows)
    outer = mul(high, places, TN) + mul(low, places, TN)
    lanes = lane_ids(field.shape)
    after = jnp.where(lanes == LANES - 1, outer, pltpu.roll(field, LANES - 1, 1))
    before = jnp.where(lanes == 0, outer, pltpu.roll(field, 1, 1))
    return after, before


def edge_lines(field):
    shape = (8, LANES)
    picks = (row_ids(shape) == 0) & (lane_ids(shape) == 0)
    picks |= (row_ids(shape) == 1) & (lane_ids(shape) == LANES - 1)
    picks = picks.astype(F32).astype(BF16)
    high, low = split(field)
    return mul(picks, high, NT) + mul(picks, low, NT)


def step_kernel(
    faces,
    velocity_in,
    earlier_in,
    y_second_in,
    y_forward_in,
    y_inverse_in,
    x_table_in,
    new_velocity,
    pressure,
    velocity,
    earlier,
    y_second,
    y_forward,
    y_inverse,
    x_table,
    edges,
    edges_in,
    below,
    above,
    partial,
    y_rows,
    gathered,
    metrics,
    factor_c,
    factor_a,
    factor_b,
    spread,
    returned,
    load_sem,
    edge_send,
    edge_recv,
    halo_send,
    halo_recv,
    out_send,
    out_recv,
    back_send,
    back_recv,
    plane_token,
    line_token,
):
    loads = [
        pltpu.make_async_copy(source, target, load_sem.at[i])
        for i, (source, target) in enumerate(
            (
                (velocity_in, velocity),
                (y_second_in, y_second),
                (earlier_in, earlier),
                (y_forward_in, y_forward),
                (x_table_in, x_table),
                (y_inverse_in, y_inverse),
            )
        )
    ]
    for load in loads:
        load.start()

    group = lax.axis_index("gx")
    layer = lax.axis_index("gz")
    me = group * 64 + layer
    y_parts = [((layer & 6) + (shift << 1)) & 6 for shift in range(4)]
    core_parts = [layer & 1, (layer & 1) ^ 1]
    x_parts = [(group + shift) & 3 for shift in range(4)]
    x_line = [x_parts[i] * 64 + layer for i in (1, 3, 2)]
    y_line = [
        group * 64 + ((layer & 56) | (y_parts[k] | core_parts[m]))
        for k, m in ((0, 1), (1, 0), (1, 1), (3, 0), (3, 1), (2, 0), (2, 1))
    ]
    z_line = [
        group * 64 + (((layer & 56) + (shift << 3)) & 56) + (layer & 7)
        for shift in (1, 7, 2, 6, 3, 5, 4)
    ]
    x_right, x_left = x_line[0], x_line[1]
    z_up = group * 64 + ((layer + 1) & 63)
    z_down = group * 64 + ((layer + 63) & 63)
    at_top = (layer & 7) == 7
    at_bottom = (layer & 7) == 0

    def tell(sem, peer):
        pl.semaphore_signal(sem, inc=1, device_id=peer, device_id_type=LOGICAL)

    def each_peer(act):
        def at_shift(shift, combos):
            z_part = ((layer & 56) + (shift << 3)) & 56
            for i, k, m in combos:
                act(x_parts[i], z_part | (y_parts[k] | core_parts[m]))

        def body(j, carry):
            at_shift(4 + (1 - 2 * (j & 1)) * ((j + 1) >> 1), Y_SHIFTS)
            return carry

        lax.fori_loop(0, 7, body, 0)
        at_shift(0, [c for c in Y_SHIFTS if c != (0, 0, 0)])

    def remote(source, target, send, recv, peer):
        return pltpu.make_async_remote_copy(
            src_ref=source,
            dst_ref=target,
            send_sem=send,
            recv_sem=recv,
            device_id=peer,
            device_id_type=LOGICAL,
        )

    barrier = pltpu.get_barrier_semaphore()

    @pl.when(at_top)
    def _():
        tell(barrier, z_up)

    @pl.when(at_bottom)
    def _():
        tell(barrier, z_down)

    for peer in y_line + x_line + z_line:
        tell(barrier, peer)
    loads[0].wait()
    for c in range(3):
        edges[0, :, c * NY : c * NY + NY] = edge_lines(velocity[c, 0])
    pl.semaphore_wait(
        barrier, 17 + jnp.where(at_top, 1, 0) + jnp.where(at_bottom, 1, 0)
    )

    halos = {}
    for c in (0, 2, 1):
        up = remote(velocity.at[c, 0], below.at[c], halo_send.at[0, c], halo_recv.at[0, c], z_up)
        down = remote(velocity.at[c, 0], above.at[c], halo_send.at[1, c], halo_recv.at[1, c], z_down)
        up.start()
        down.start()
        halos[c] = (up, down)

    def send_edges(k, width):
        copies = []
        for side, peer in enumerate((x_right, x_left)):
            copies.append(
                remote(
                    edges.at[k, :, pl.ds(0, width)],
                    edges_in.at[k, side, :, pl.ds(0, width)],
                    edge_send.at[k, side],
                    edge_recv.at[k, side],
                    peer,
                )
            )
            copies[-1].start()
        return copies

    def edge_pair(k, first):
        part = slice(first, first + NY)
        return jnp.concatenate([edges_in[k, 0, :, part], edges_in[k, 1, :, part]], 0)

    velocity_edges = send_edges(0, 3 * NY)
    for peer in y_line:
        tell(plane_token, peer)

    u = velocity[0, 0]
    v = velocity[1, 0]
    loads[1].wait()
    loads[2].wait()
    for c in (0, 2, 1):
        field = velocity[c, 0]
        after, before = y_neighbours(field)
        bend = table_times(y_second, field) - 2.0 * field
        partial[c] = field + TIME_STEP * (
            EARLIER_WEIGHT * earlier[c, 0].astype(F32)
            + VISCOUS_WEIGHT * bend
            - ADVECT_WEIGHT * (v * (0.5 * (after - before)))
        )

    pl.semaphore_wait(plane_token, 7)
    for peer in x_line:
        tell(line_token, peer)

    for copy in velocity_edges:
        copy.wait()
    for c in (0, 2, 1):
        after, before = lined_x(velocity[c, 0], edge_pair(0, c * NY))
        partial[c] = partial[c] + TIME_STEP * (
            VISCOUS_WEIGHT * (after + before) - ADVECT_WEIGHT * (u * (0.5 * (after - before)))
        )
    loads[3].wait()

    lower = faces[0, layer]
    upper = faces[1, layer]
    metric = 0.5 * (lower + upper)
    w = velocity[2, 0]

    def predict(c):
        for copy in halos[c]:
            copy.wait()
        field = velocity[c, 0]
        after = jnp.where(layer == NZ - 1, 0.0, above[c])
        before = jnp.where(layer == 0, 0.0, below[c])
        bend = metric * (upper * (after - field) - lower * (field - before))
        predicted = partial[c] + TIME_STEP * (
            VISCOUS_WEIGHT * bend - ADVECT_WEIGHT * (w * (metric * (0.5 * (after - before))))
        )
        partial[c] = predicted
        return predicted

    def send_rows(slot, field):
        y_rows[slot] = table_times(y_forward, field)

        def send(px, pz):
            peer = px * 64 + pz
            remote(
                y_rows.at[slot, pl.ds(peer, 1)],
                gathered.at[slot, group, pl.ds(layer, 1)],
                out_send.at[slot],
                out_recv.at[slot],
                peer,
            ).start()

        each_peer(send)
        gathered[slot, group, pl.ds(layer, 1)] = y_rows[slot, pl.ds(me, 1)]

    predicted_u = predict(0)
    edges[1, :, :NY] = edge_lines(predicted_u)
    u_edges = send_edges(1, NY)
    predicted_w = predict(2)
    pl.semaphore_wait(line_token, 3)
    send_rows(0, predicted_w)
    after, before = y_neighbours(predict(1))
    flow = after - before
    for copy in u_edges:
        copy.wait()
    after, before = lined_x(partial[0], edge_pair(1, 0))
    send_rows(1, 0.5 * (flow + (after - before)))

    k_y = me.astype(F32) * (math.pi / NY)
    k_x = lane_ids((1, NX)).astype(F32) * (math.pi / NX)
    eigen = k_y * k_y + k_x * k_x
    ratio = jnp.zeros((1, NX), F32)
    for z in range(NZ):
        lower = faces[0, z]
        upper = faces[1, z]
        metrics[pl.ds(z, 1)] = jnp.full((1, LANES), 0.5 * (lower + upper), F32)
        per_metric = 2.0 / jnp.full((1, NX), lower + upper, F32)
        inverse = 1.0 / (-(lower + upper) - eigen * per_metric - lower * ratio)
        ratio = upper * inverse
        factor_c[pl.ds(z, 1)] = ratio
        factor_a[pl.ds(z, 1)] = lower * inverse
        factor_b[pl.ds(z, 1)] = (per_metric * inverse) * (1.0 / TIME_STEP)
    metric_rows = jnp.concatenate([metrics[...]] * 4, 1)
    loads[4].wait()
    loads[5].wait()

    others = returned.at[0, pl.ds(0, PEERS - 1)]

    def finish(sem):
        pltpu.make_async_copy(others, others, sem).wait()

    def lines(slot):
        return jnp.concatenate([gathered[slot, part] for part in range(4)], 1)

    finish(out_recv.at[0])
    source = z_slope(lines(0), metric_rows)
    finish(out_recv.at[1])
    source = source + lines(1)
    factor_b[...] = factor_b[...] * times_table(source, x_table, NT)
    value = jnp.zeros((1, NX), F32)
    for z in range(NZ):
        value = factor_b[pl.ds(z, 1)] - factor_a[pl.ds(z, 1)] * value
        factor_b[pl.ds(z, 1)] = value
    value = jnp.zeros((1, NX), F32)
    for z in reversed(range(NZ)):
        value = factor_b[pl.ds(z, 1)] - factor_c[pl.ds(z, 1)] * value
        factor_b[pl.ds(z, 1)] = value
    solved = times_table(factor_b[...], x_table, NN)
    for slot, lined in ((0, solved), (1, z_slope(solved, metric_rows))):
        for part in range(4):
            spread[slot, part] = lined[:, part * LANES : part * LANES + LANES]

        def send_back(px, pz):
            remote(
                spread.at[slot, px, pl.ds(pz, 1)],
                returned.at[slot, pl.ds(me, 1)],
                back_send.at[slot],
                back_recv.at[slot],
                px * 64 + pz,
            ).start()

        each_peer(send_back)
        returned[slot, pl.ds(me, 1)] = spread[slot, group, pl.ds(layer, 1)]

    finish(back_recv.at[0])
    rows = returned[0]
    edges[2, :, :NY] = edge_lines(rows)
    p_edges = send_edges(2, NY)
    field = table_times(y_inverse, rows)
    pressure[0] = field
    after, before = y_neighbours(field)
    new_velocity[1, 0] = partial[1] - (0.5 * TIME_STEP) * (after - before)
    for copy in p_edges:
        copy.wait()
    after, before = lined_x(rows, edge_pair(2, 0))
    new_velocity[0, 0] = partial[0] - TIME_STEP * table_times(y_inverse, 0.5 * (after - before))
    finish(back_recv.at[1])
    new_velocity[2, 0] = partial[2] - TIME_STEP * table_times(y_inverse, returned[1])
    for slot in range(2):
        finish(out_send.at[slot])
        finish(back_send.at[slot])


def per_device(velocity, earlier_term, face_metric):
    y_cosines = cosine_table(NY)
    y_squares = (np.arange(NY) * (math.pi / NY)) ** 2
    y_second = -(y_cosines.T * y_squares) @ y_cosines
    vmem = pl.BlockSpec(memory_space=pltpu.VMEM)
    hbm = pl.BlockSpec(memory_space=pltpu.HBM)
    dma = pltpu.SemaphoreType.DMA
    return pl.pallas_call(
        step_kernel,
        out_shape=(
            jax.ShapeDtypeStruct(velocity.shape, F32),
            jax.ShapeDtypeStruct(velocity.shape[1:], F32),
        ),
        in_specs=[pl.BlockSpec(memory_space=pltpu.SMEM)] + [hbm] * 6,
        out_specs=(vmem, vmem),
        scratch_shapes=[
            pltpu.VMEM((3, 1, NY, LANES), F32),
            pltpu.VMEM((3, 1, NY, LANES), BF16),
            pltpu.VMEM((2, NY, NY), BF16),
            pltpu.VMEM((2, NY, NY), BF16),
            pltpu.VMEM((2, NY, NY), BF16),
            pltpu.VMEM((2, NX, NX), BF16),
            pltpu.VMEM((3, 8, 3 * NY), F32),
            pltpu.VMEM((3, 2, 8, 3 * NY), F32),
            pltpu.VMEM((3, NY, LANES), F32),
            pltpu.VMEM((3, NY, LANES), F32),
            pltpu.VMEM((3, NY, LANES), F32),
            pltpu.VMEM((2, NY, LANES), F32),
            pltpu.VMEM((2, 4, NZ, LANES), F32),
            pltpu.VMEM((NZ, LANES), F32),
            pltpu.VMEM((NZ, NX), F32),
            pltpu.VMEM((NZ, NX), F32),
            pltpu.VMEM((NZ, NX), F32),
            pltpu.VMEM((2, 4, NZ, LANES), F32),
            pltpu.VMEM((2, NY, LANES), F32),
            dma((6,)),
            dma((3, 2)),
            dma((3, 2)),
            dma((2, 3)),
            dma((2, 3)),
            dma((2,)),
            dma((2,)),
            dma((2,)),
            dma((2,)),
            pltpu.SemaphoreType.REGULAR,
            pltpu.SemaphoreType.REGULAR,
        ],
        compiler_params=pltpu.CompilerParams(
            collective_id=0, has_side_effects=True
        ),
    )(
        face_metric,
        velocity,
        earlier_term,
        jnp.asarray(halves(y_second)),
        jnp.asarray(halves(y_cosines)),
        jnp.asarray(halves(y_cosines.T)),
        jnp.asarray(halves(cosine_table(NX))),
    )


def solution(mesh):
    placed = (P(None, "gz", None, "gx"), P(None, "gz", None, "gx"), P())
    return jax.shard_map(
        per_device,
        mesh=mesh,
        in_specs=placed,
        out_specs=(P(None, "gz", None, "gx"), P("gz", None, "gx")),
        check_vma=False,
    )
```

time: 51.9 us -> 44.3 us (0.85)
  Pallas kernels: 48.6 us -> 41 us
    pallas_call x1, Pallas kernels: 48.6 us -> 41 us  [per_device(): pl.pallas_call(step_kernel, out_shape=(jax.ShapeDtypeStruct(velocity.shap...]
where the time goes in v3:
time: 44.3 us; the launch traced here: 44.1 us
  Pallas kernels  41 us (93%)
  local copies, waits for them, and re-layouts  2.46 us (6%)
  between operations  0.65 us (1%)
    pallas_call x1, Pallas kernels, per_device(): pl.pallas_call(step_kernel, out_shape=(jax.ShapeDtypeStruct(velocity.shap...  41 us
    unnamed x4, local copies, waits for them, and re-layouts  2.46 us

profile of v3, /device:TPU:1, one launch (start us, length us, event | category | flops | bytes accessed | tf_op | source)
XLA Modules:
  0.0 44.1 jit_solution(1883945103748370840)
XLA Ops:
  0.6 41.0 %shard_map.86 = (f32[3,1,256,128]{3,2,1,0:T(8,128)}, f32[1,256,128]{2,1,0:T(8,128)}) custom-call(f32[2,64]{1,0:T(2,128)} %faces.1, f32[3,1,256,128]{3,2,1,0:T(8,128)} %velocity_in.1, bf16[3,1,256,128]{3,2,1,0:T(8,128)(2,1)} %earlier_in.1, bf16[2,256,256]{2,1,0:T(8,128)(2,1)} %constant.8.clone.y_second_in, bf16[2,256,256]{2,1,0:T(8,128)(2,1)} %constant.9.clone.y_forward_in, ...), custom_call_target="tpu_custom_call" | custom-call | tf_op jit(solution)/shard_map/pallas_call | solution.py:427
  41.6 0.0 copy-start
  41.7 1.8 %copy.11 = f32[3,1,256,128]{3,2,1,0:T(8,128)} copy(f32[3,1,256,128]{3,2,1,0:T(8,128)} %get-tuple-element.4) | data formatting | bytes 786432
  43.5 0.0 copy-done
  43.5 0.7 %copy.12 = f32[1,256,128]{2,1,0:T(8,128)} copy(f32[1,256,128]{2,1,0:T(8,128)S(1)} %copy-done) | data formatting | bytes 262144
Async XLA Ops:
  41.6 1.8 %copy-start = (f32[1,256,128]{2,1,0:T(8,128)S(1)}, f32[1,256,128]{2,1,0:T(8,128)}, u32[]{:S(2)}) copy-start(f32[1,256,128]{2,1,0:T(8,128)} %get-tuple-element.5) | copy-start | bytes 393220

commit v4 on v3

--- a/solution.py
+++ b/solution.py
@@ -132,6 +132,7 @@
     x_table,
     edges,
     edges_in,
+    edges_z,
     below,
     above,
     partial,
@@ -159,7 +160,9 @@
         pltpu.make_async_copy(source, target, load_sem.at[i])
         for i, (source, target) in enumerate(
             (
-                (velocity_in, velocity),
+                (velocity_in.at[0], velocity.at[0]),
+                (velocity_in.at[2], velocity.at[2]),
+                (velocity_in.at[1], velocity.at[1]),
                 (y_second_in, y_second),
                 (earlier_in, earlier),
                 (y_forward_in, y_forward),
@@ -230,20 +233,13 @@
 
     for peer in y_line + x_line + z_line:
         tell(barrier, peer)
-    loads[0].wait()
+    for i in range(3):
+        loads[i].wait()
     for c in range(3):
         edges[0, :, c * NY : c * NY + NY] = edge_lines(velocity[c, 0])
     pl.semaphore_wait(
         barrier, 17 + jnp.where(at_top, 1, 0) + jnp.where(at_bottom, 1, 0)
     )
-
-    halos = {}
-    for c in (0, 2, 1):
-        up = remote(velocity.at[c, 0], below.at[c], halo_send.at[0, c], halo_recv.at[0, c], z_up)
-        down = remote(velocity.at[c, 0], above.at[c], halo_send.at[1, c], halo_recv.at[1, c], z_down)
-        up.start()
-        down.start()
-        halos[c] = (up, down)
 
     def send_edges(k, width):
         copies = []
@@ -265,13 +261,28 @@
         return jnp.concatenate([edges_in[k, 0, :, part], edges_in[k, 1, :, part]], 0)
 
     velocity_edges = send_edges(0, 3 * NY)
+    layer_edges = []
+    for side, peer in enumerate((z_up, z_down)):
+        layer_edges.append(
+            remote(
+                edges.at[0], edges_z.at[side], edge_send.at[3, side], edge_recv.at[3, side], peer
+            )
+        )
+        layer_edges[-1].start()
+    halos = {}
+    for c in (2, 0, 1):
+        up = remote(velocity.at[c, 0], below.at[c], halo_send.at[0, c], halo_recv.at[0, c], z_up)
+        down = remote(velocity.at[c, 0], above.at[c], halo_send.at[1, c], halo_recv.at[1, c], z_down)
+        up.start()
+        down.start()
+        halos[c] = (up, down)
     for peer in y_line:
         tell(plane_token, peer)
 
     u = velocity[0, 0]
     v = velocity[1, 0]
-    loads[1].wait()
-    loads[2].wait()
+    loads[3].wait()
+    loads[4].wait()
     for c in (0, 2, 1):
         field = velocity[c, 0]
         after, before = y_neighbours(field)
@@ -286,32 +297,49 @@
     for peer in x_line:
         tell(line_token, peer)
 
-    for copy in velocity_edges:
-        copy.wait()
-    for c in (0, 2, 1):
-        after, before = lined_x(velocity[c, 0], edge_pair(0, c * NY))
-        partial[c] = partial[c] + TIME_STEP * (
-            VISCOUS_WEIGHT * (after + before) - ADVECT_WEIGHT * (u * (0.5 * (after - before)))
-        )
-    loads[3].wait()
-
     lower = faces[0, layer]
     upper = faces[1, layer]
     metric = 0.5 * (lower + upper)
     w = velocity[2, 0]
 
+    def with_z(base, field, below_it, above_it, drift):
+        after = jnp.where(layer == NZ - 1, 0.0, above_it)
+        before = jnp.where(layer == 0, 0.0, below_it)
+        bend = metric * (upper * (after - field) - lower * (field - before))
+        return base + TIME_STEP * (
+            VISCOUS_WEIGHT * bend - ADVECT_WEIGHT * (drift * (metric * (0.5 * (after - before))))
+        )
+
+    def add_x(c):
+        after, before = lined_x(velocity[c, 0], edge_pair(0, c * NY))
+        partial[c] = partial[c] + TIME_STEP * (
+            VISCOUS_WEIGHT * (after + before) - ADVECT_WEIGHT * (u * (0.5 * (after - before)))
+        )
+
     def predict(c):
         for copy in halos[c]:
             copy.wait()
-        field = velocity[c, 0]
-        after = jnp.where(layer == NZ - 1, 0.0, above[c])
-        before = jnp.where(layer == 0, 0.0, below[c])
-        bend = metric * (upper * (after - field) - lower * (field - before))
-        predicted = partial[c] + TIME_STEP * (
-            VISCOUS_WEIGHT * bend - ADVECT_WEIGHT * (w * (metric * (0.5 * (after - before))))
-        )
+        predicted = with_z(partial[c], velocity[c, 0], below[c], above[c], w)
         partial[c] = predicted
         return predicted
+
+    for copy in velocity_edges:
+        copy.wait()
+    add_x(0)
+    own = edge_lines(partial[0])
+    for copy in layer_edges:
+        copy.wait()
+    edges[1, :, :NY] = with_z(
+        own,
+        edges[0, :, :NY],
+        edges_z[0, :, :NY],
+        edges_z[1, :, :NY],
+        edges[0, :, 2 * NY :],
+    )
+    u_edges = send_edges(1, NY)
+    add_x(2)
+    add_x(1)
+    loads[5].wait()
 
     def send_rows(slot, field):
         y_rows[slot] = table_times(y_forward, field)
@@ -329,17 +357,15 @@
         each_peer(send)
         gathered[slot, group, pl.ds(layer, 1)] = y_rows[slot, pl.ds(me, 1)]
 
-    predicted_u = predict(0)
-    edges[1, :, :NY] = edge_lines(predicted_u)
-    u_edges = send_edges(1, NY)
     predicted_w = predict(2)
     pl.semaphore_wait(line_token, 3)
     send_rows(0, predicted_w)
-    after, before = y_neighbours(predict(1))
-    flow = after - before
+    predicted_u = predict(0)
     for copy in u_edges:
         copy.wait()
-    after, before = lined_x(partial[0], edge_pair(1, 0))
+    after, before = lined_x(predicted_u, edge_pair(1, 0))
+    flow = after - before
+    after, before = y_neighbours(predict(1))
     send_rows(1, 0.5 * (flow + (after - before)))
 
     k_y = me.astype(F32) * (math.pi / NY)
@@ -357,8 +383,8 @@
         factor_a[pl.ds(z, 1)] = lower * inverse
         factor_b[pl.ds(z, 1)] = (per_metric * inverse) * (1.0 / TIME_STEP)
     metric_rows = jnp.concatenate([metrics[...]] * 4, 1)
-    loads[4].wait()
-    loads[5].wait()
+    loads[6].wait()
+    loads[7].wait()
 
     others = returned.at[0, pl.ds(0, PEERS - 1)]
 
@@ -417,6 +443,17 @@
         finish(back_send.at[slot])
 
 
+def publish_kernel(step_in, pressure_in, step_out, pressure_out, sems):
+    copies = (
+        pltpu.make_async_copy(step_in, step_out, sems.at[0]),
+        pltpu.make_async_copy(pressure_in, pressure_out, sems.at[1]),
+    )
+    for copy in copies:
+        copy.start()
+    for copy in copies:
+        copy.wait()
+
+
 def per_device(velocity, earlier_term, face_metric):
     y_cosines = cosine_table(NY)
     y_squares = (np.arange(NY) * (math.pi / NY)) ** 2
@@ -424,7 +461,18 @@
     vmem = pl.BlockSpec(memory_space=pltpu.VMEM)
     hbm = pl.BlockSpec(memory_space=pltpu.HBM)
     dma = pltpu.SemaphoreType.DMA
-    return pl.pallas_call(
+    arrays = [
+        pltpu.with_memory_space_constraint(array, pltpu.HBM)
+        for array in (
+            velocity,
+            earlier_term,
+            jnp.asarray(halves(y_second)),
+            jnp.asarray(halves(y_cosines)),
+            jnp.asarray(halves(y_cosines.T)),
+            jnp.asarray(halves(cosine_table(NX))),
+        )
+    ]
+    stepped = pl.pallas_call(
         step_kernel,
         out_shape=(
             jax.ShapeDtypeStruct(velocity.shape, F32),
@@ -441,6 +489,7 @@
             pltpu.VMEM((2, NX, NX), BF16),
             pltpu.VMEM((3, 8, 3 * NY), F32),
             pltpu.VMEM((3, 2, 8, 3 * NY), F32),
+            pltpu.VMEM((2, 8, 3 * NY), F32),
             pltpu.VMEM((3, NY, LANES), F32),
             pltpu.VMEM((3, NY, LANES), F32),
             pltpu.VMEM((3, NY, LANES), F32),
@@ -452,9 +501,9 @@
             pltpu.VMEM((NZ, NX), F32),
             pltpu.VMEM((2, 4, NZ, LANES), F32),
             pltpu.VMEM((2, NY, LANES), F32),
-            dma((6,)),
-            dma((3, 2)),
-            dma((3, 2)),
+            dma((8,)),
+            dma((4, 2)),
+            dma((4, 2)),
             dma((2, 3)),
             dma((2, 3)),
             dma((2,)),
@@ -465,17 +514,17 @@
             pltpu.SemaphoreType.REGULAR,
         ],
         compiler_params=pltpu.CompilerParams(
-            collective_id=0, has_side_effects=True
+            collective_id=0, has_side_effects=True, vmem_limit_bytes=16 << 20
         ),
-    )(
-        face_metric,
-        velocity,
-        earlier_term,
-        jnp.asarray(halves(y_second)),
-        jnp.asarray(halves(y_cosines)),
-        jnp.asarray(halves(y_cosines.T)),
-        jnp.asarray(halves(cosine_table(NX))),
-    )
+    )(pltpu.with_memory_space_constraint(face_metric, pltpu.HBM), *arrays)
+    return pl.pallas_call(
+        publish_kernel,
+        out_shape=tuple(jax.ShapeDtypeStruct(a.shape, a.dtype) for a in stepped),
+        in_specs=[vmem, vmem],
+        out_specs=(hbm, hbm),
+        scratch_shapes=[dma((2,))],
+        compiler_params=pltpu.CompilerParams(vmem_limit_bytes=4 << 20),
+    )(*stepped)
 
 
 def solution(mesh):

time: 44.3 us -> 41.5 us (0.937)
  local copies, waits for them, and re-layouts: 2.46 us -> 0 us
    unnamed x4 -> x0, local copies, waits for them, and re-layouts: 2.46 us -> none
    pallas_call x1, Pallas kernels: 41 us -> 40 us  [per_device(): pl.pallas_call(step_kernel, out_shape=(jax.ShapeDtypeStruct(velocity.shap...]
    pallas_call x0 -> x1, Pallas kernels: none -> 0.8 us  [per_device(): pl.pallas_call(publish_kernel, out_shape=tuple((jax.ShapeDtypeStruct(a.sh...]
where the time goes in v4:
time: 41.5 us; the launch traced here: 41.4 us
  Pallas kernels  40.8 us (98%)
  between operations  0.64 us (2%)
    pallas_call x1, Pallas kernels, per_device(): pl.pallas_call(step_kernel, out_shape=(jax.ShapeDtypeStruct(velocity.shap...  40 us

profile of v4, /device:TPU:1, one launch (start us, length us, event | category | flops | bytes accessed | tf_op | source)
XLA Modules:
  0.0 41.4 jit_solution(17149702343828609720)
XLA Ops:
  0.6 40.0 %shard_map.86 = (f32[3,1,256,128]{3,2,1,0:T(8,128)S(1)}, f32[1,256,128]{2,1,0:T(8,128)S(1)}) custom-call(f32[2,64]{1,0:T(2,128)} %faces.1, f32[3,1,256,128]{3,2,1,0:T(8,128)} %velocity_in.1, bf16[3,1,256,128]{3,2,1,0:T(8,128)(2,1)} %earlier_in.1, bf16[2,256,256]{2,1,0:T(8,128)(2,1)} %constant.8.clone.y_second_in, ...), custom_call_target="tpu_custom_call" | custom-call | tf_op jit(solution)/shard_map/pallas_call | solution.py:475
  40.6 0.8 %shard_map.87 = (f32[3,1,256,128]{3,2,1,0:T(8,128)}, f32[1,256,128]{2,1,0:T(8,128)}) custom-call(f32[3,1,256,128]{3,2,1,0:T(8,128)S(1)} %get-tuple-element.4.step_in, f32[1,256,128]{2,1,0:T(8,128)S(1)} %get-tuple-element.5.pressure_in), custom_call_target="tpu_custom_call" | custom-call | tf_op jit(solution)/shard_map/pallas_call | solution.py:520

commit v5 on v4

--- a/solution.py
+++ b/solution.py
@@ -23,7 +23,23 @@
 NN = (((1,), (0,)), ((), ()))
 NT = (((1,), (1,)), ((), ()))
 TN = (((0,), (0,)), ((), ()))
-Y_SHIFTS = [(i, k, m) for k in (2, 1, 3, 0) for i in (2, 1, 3, 0) for m in (1, 0)]
+
+
+def hops(shift):
+    return min(shift[0], 4 - shift[0]) + min(shift[1], 4 - shift[1]) + min(shift[2], 8 - shift[2])
+
+
+SHIFTS = sorted(
+    (
+        (i, k, j, m)
+        for m in (1, 0)
+        for j in (4, 3, 5, 2, 6, 1, 7, 0)
+        for k in (2, 1, 3, 0)
+        for i in (2, 1, 3, 0)
+        if (i, k, j, m) != (0, 0, 0, 0)
+    ),
+    key=lambda shift: -hops(shift),
+)
 
 
 def cosine_table(extent):
@@ -171,7 +187,7 @@
             )
         )
     ]
-    for load in loads:
+    for load in loads[:3]:
         load.start()
 
     group = lax.axis_index("gx")
@@ -198,18 +214,11 @@
     def tell(sem, peer):
         pl.semaphore_signal(sem, inc=1, device_id=peer, device_id_type=LOGICAL)
 
+    z_parts = [((layer & 56) + (shift << 3)) & 56 for shift in range(8)]
+
     def each_peer(act):
-        def at_shift(shift, combos):
-            z_part = ((layer & 56) + (shift << 3)) & 56
-            for i, k, m in combos:
-                act(x_parts[i], z_part | (y_parts[k] | core_parts[m]))
-
-        def body(j, carry):
-            at_shift(4 + (1 - 2 * (j & 1)) * ((j + 1) >> 1), Y_SHIFTS)
-            return carry
-
-        lax.fori_loop(0, 7, body, 0)
-        at_shift(0, [c for c in Y_SHIFTS if c != (0, 0, 0)])
+        for i, k, j, m in SHIFTS:
+            act(x_parts[i], z_parts[j] | (y_parts[k] | core_parts[m]))
 
     def remote(source, target, send, recv, peer):
         return pltpu.make_async_remote_copy(
@@ -235,6 +244,8 @@
         tell(barrier, peer)
     for i in range(3):
         loads[i].wait()
+    for load in loads[3:]:
+        load.start()
     for c in range(3):
         edges[0, :, c * NY : c * NY + NY] = edge_lines(velocity[c, 0])
     pl.semaphore_wait(
@@ -432,12 +443,12 @@
     pressure[0] = field
     after, before = y_neighbours(field)
     new_velocity[1, 0] = partial[1] - (0.5 * TIME_STEP) * (after - before)
+    finish(back_recv.at[1])
+    new_velocity[2, 0] = partial[2] - TIME_STEP * table_times(y_inverse, returned[1])
     for copy in p_edges:
         copy.wait()
     after, before = lined_x(rows, edge_pair(2, 0))
     new_velocity[0, 0] = partial[0] - TIME_STEP * table_times(y_inverse, 0.5 * (after - before))
-    finish(back_recv.at[1])
-    new_velocity[2, 0] = partial[2] - TIME_STEP * table_times(y_inverse, returned[1])
     for slot in range(2):
         finish(out_send.at[slot])
         finish(back_send.at[slot])

time: 41.5 us -> 40.5 us (0.976)
  Pallas kernels: 40.8 us -> 39.7 us
    pallas_call x1, Pallas kernels: 40 us -> 38.9 us  [per_device(): pl.pallas_call(step_kernel, out_shape=(jax.ShapeDtypeStruct(velocity.shap...]
where the time goes in v5:
time: 40.5 us; the launch traced here: 40.4 us
  Pallas kernels  39.7 us (98%)
  between operations  0.64 us (2%)
    pallas_call x1, Pallas kernels, per_device(): pl.pallas_call(step_kernel, out_shape=(jax.ShapeDtypeStruct(velocity.shap...  38.9 us

profile of v5, /device:TPU:1, one launch (start us, length us, event | category | flops | bytes accessed | tf_op | source)
XLA Modules:
  0.0 40.4 jit_solution(14802297477921077183)
XLA Ops:
  0.6 38.9 %shard_map.86 = (f32[3,1,256,128]{3,2,1,0:T(8,128)S(1)}, f32[1,256,128]{2,1,0:T(8,128)S(1)}) custom-call(f32[2,64]{1,0:T(2,128)} %faces.1, f32[3,1,256,128]{3,2,1,0:T(8,128)} %velocity_in.1, bf16[3,1,256,128]{3,2,1,0:T(8,128)(2,1)} %earlier_in.1, bf16[2,256,256]{2,1,0:T(8,128)(2,1)} %constant.8.clone.y_second_in, ...), custom_call_target="tpu_custom_call" | custom-call | tf_op jit(solution)/shard_map/pallas_call | solution.py:486
  39.5 0.8 %shard_map.87 = (f32[3,1,256,128]{3,2,1,0:T(8,128)}, f32[1,256,128]{2,1,0:T(8,128)}) custom-call(f32[3,1,256,128]{3,2,1,0:T(8,128)S(1)} %get-tuple-element.4.step_in, f32[1,256,128]{2,1,0:T(8,128)S(1)} %get-tuple-element.5.pressure_in), custom_call_target="tpu_custom_call" | custom-call | tf_op jit(solution)/shard_map/pallas_call | solution.py:531

commit v6 on v5

--- a/solution.py
+++ b/solution.py
@@ -158,6 +158,7 @@
     factor_c,
     factor_a,
     factor_b,
+    middle,
     spread,
     returned,
     load_sem,
@@ -382,17 +383,26 @@
     k_y = me.astype(F32) * (math.pi / NY)
     k_x = lane_ids((1, NX)).astype(F32) * (math.pi / NX)
     eigen = k_y * k_y + k_x * k_x
-    ratio = jnp.zeros((1, NX), F32)
-    for z in range(NZ):
-        lower = faces[0, z]
-        upper = faces[1, z]
-        metrics[pl.ds(z, 1)] = jnp.full((1, LANES), 0.5 * (lower + upper), F32)
-        per_metric = 2.0 / jnp.full((1, NX), lower + upper, F32)
-        inverse = 1.0 / (-(lower + upper) - eigen * per_metric - lower * ratio)
-        ratio = upper * inverse
+
+    def factor_row(z, ratio, inner, outer):
+        total = faces[0, z] + faces[1, z]
+        metrics[pl.ds(z, 1)] = jnp.full((1, LANES), 0.5 * total, F32)
+        per_metric = 2.0 / jnp.full((1, NX), total, F32)
+        inverse = 1.0 / (-total - eigen * per_metric - inner * ratio)
+        ratio = outer * inverse
         factor_c[pl.ds(z, 1)] = ratio
-        factor_a[pl.ds(z, 1)] = lower * inverse
+        factor_a[pl.ds(z, 1)] = inner * inverse
         factor_b[pl.ds(z, 1)] = (per_metric * inverse) * (1.0 / TIME_STEP)
+        return ratio
+
+    half = NZ // 2
+    low_ratio = jnp.zeros((1, NX), F32)
+    high_ratio = jnp.zeros((1, NX), F32)
+    for z in range(half):
+        low_ratio = factor_row(z, low_ratio, faces[0, z], faces[1, z])
+        mirror = NZ - 1 - z
+        high_ratio = factor_row(mirror, high_ratio, faces[1, mirror], faces[0, mirror])
+    middle[...] = 1.0 / (1.0 - low_ratio * high_ratio)
     metric_rows = jnp.concatenate([metrics[...]] * 4, 1)
     loads[6].wait()
     loads[7].wait()
@@ -410,14 +420,24 @@
     finish(out_recv.at[1])
     source = source + lines(1)
     factor_b[...] = factor_b[...] * times_table(source, x_table, NT)
-    value = jnp.zeros((1, NX), F32)
-    for z in range(NZ):
-        value = factor_b[pl.ds(z, 1)] - factor_a[pl.ds(z, 1)] * value
-        factor_b[pl.ds(z, 1)] = value
-    value = jnp.zeros((1, NX), F32)
-    for z in reversed(range(NZ)):
-        value = factor_b[pl.ds(z, 1)] - factor_c[pl.ds(z, 1)] * value
-        factor_b[pl.ds(z, 1)] = value
+    low = jnp.zeros((1, NX), F32)
+    high = jnp.zeros((1, NX), F32)
+    for z in range(half):
+        mirror = NZ - 1 - z
+        low = factor_b[pl.ds(z, 1)] - factor_a[pl.ds(z, 1)] * low
+        high = factor_b[pl.ds(mirror, 1)] - factor_a[pl.ds(mirror, 1)] * high
+        factor_b[pl.ds(z, 1)] = low
+        factor_b[pl.ds(mirror, 1)] = high
+    low = (low - factor_c[pl.ds(half - 1, 1)] * high) * middle[...]
+    high = high - factor_c[pl.ds(half, 1)] * low
+    factor_b[pl.ds(half - 1, 1)] = low
+    factor_b[pl.ds(half, 1)] = high
+    for z in reversed(range(half - 1)):
+        mirror = NZ - 1 - z
+        low = factor_b[pl.ds(z, 1)] - factor_c[pl.ds(z, 1)] * low
+        high = factor_b[pl.ds(mirror, 1)] - factor_c[pl.ds(mirror, 1)] * high
+        factor_b[pl.ds(z, 1)] = low
+        factor_b[pl.ds(mirror, 1)] = high
     solved = times_table(factor_b[...], x_table, NN)
     for slot, lined in ((0, solved), (1, z_slope(solved, metric_rows))):
         for part in range(4):
@@ -441,14 +461,22 @@
     p_edges = send_edges(2, NY)
     field = table_times(y_inverse, rows)
     pressure[0] = field
+    lanes = lane_ids(rows.shape)
+    after = jnp.where(lanes == LANES - 1, 0.0, pltpu.roll(rows, LANES - 1, 1))
+    before = jnp.where(lanes == 0, 0.0, pltpu.roll(rows, 1, 1))
+    inner_slope = table_times(y_inverse, 0.5 * (after - before))
     after, before = y_neighbours(field)
     new_velocity[1, 0] = partial[1] - (0.5 * TIME_STEP) * (after - before)
     finish(back_recv.at[1])
     new_velocity[2, 0] = partial[2] - TIME_STEP * table_times(y_inverse, returned[1])
     for copy in p_edges:
         copy.wait()
-    after, before = lined_x(rows, edge_pair(2, 0))
-    new_velocity[0, 0] = partial[0] - TIME_STEP * table_times(y_inverse, 0.5 * (after - before))
+    shape = (16, LANES)
+    places = jnp.where((row_ids(shape) == 8) & (lane_ids(shape) == LANES - 1), 0.5, 0.0)
+    places = jnp.where((row_ids(shape) == 1) & (lane_ids(shape) == 0), -0.5, places).astype(BF16)
+    high, low = split(times_table(edge_pair(2, 0), y_inverse, NT))
+    slope = inner_slope + (mul(high, places, TN) + mul(low, places, TN))
+    new_velocity[0, 0] = partial[0] - TIME_STEP * slope
     for slot in range(2):
         finish(out_send.at[slot])
         finish(back_send.at[slot])
@@ -510,6 +538,7 @@
             pltpu.VMEM((NZ, NX), F32),
             pltpu.VMEM((NZ, NX), F32),
             pltpu.VMEM((NZ, NX), F32),
+            pltpu.VMEM((1, NX), F32),
             pltpu.VMEM((2, 4, NZ, LANES), F32),
             pltpu.VMEM((2, NY, LANES), F32),
             dma((8,)),

time: 40.5 us -> 40.3 us (level)
  no operation moved by 1% of the time
where the time goes in v6:
time: 40.3 us; the launch traced here: 40.1 us
  Pallas kernels  39.5 us (98%)
  between operations  0.64 us (2%)
    pallas_call x1, Pallas kernels, per_device(): pl.pallas_call(step_kernel, out_shape=(jax.ShapeDtypeStruct(velocity.shap...  38.7 us

profile of v6, /device:TPU:1, one launch (start us, length us, event | category | flops | bytes accessed | tf_op | source)
XLA Modules:
  0.0 40.1 jit_solution(17544154906461986751)
XLA Ops:
  0.6 38.7 %shard_map.86 = (f32[3,1,256,128]{3,2,1,0:T(8,128)S(1)}, f32[1,256,128]{2,1,0:T(8,128)S(1)}) custom-call(f32[2,64]{1,0:T(2,128)} %faces.1, f32[3,1,256,128]{3,2,1,0:T(8,128)} %velocity_in.1, bf16[3,1,256,128]{3,2,1,0:T(8,128)(2,1)} %earlier_in.1, bf16[2,256,256]{2,1,0:T(8,128)(2,1)} %constant.8.clone.y_second_in, ...), custom_call_target="tpu_custom_call" | custom-call | tf_op jit(solution)/shard_map/pallas_call | solution.py:514
  39.3 0.8 %shard_map.87 = (f32[3,1,256,128]{3,2,1,0:T(8,128)}, f32[1,256,128]{2,1,0:T(8,128)}) custom-call(f32[3,1,256,128]{3,2,1,0:T(8,128)S(1)} %get-tuple-element.4.step_in, f32[1,256,128]{2,1,0:T(8,128)S(1)} %get-tuple-element.5.pressure_in), custom_call_target="tpu_custom_call" | custom-call | tf_op jit(solution)/shard_map/pallas_call | solution.py:560

commit v7 on v6

--- a/solution.py
+++ b/solution.py
@@ -439,7 +439,8 @@
         factor_b[pl.ds(z, 1)] = low
         factor_b[pl.ds(mirror, 1)] = high
     solved = times_table(factor_b[...], x_table, NN)
-    for slot, lined in ((0, solved), (1, z_slope(solved, metric_rows))):
+    for slot in range(2):
+        lined = z_slope(solved, metric_rows) if slot else solved
         for part in range(4):
             spread[slot, part] = lined[:, part * LANES : part * LANES + LANES]
 

time: 40.3 us -> 40.3 us (level)
  no operation moved by 1% of the time
where the time goes in v7:
time: 40.3 us; the launch traced here: 40.1 us
  Pallas kernels  39.5 us (98%)
  between operations  0.64 us (2%)
    pallas_call x1, Pallas kernels, per_device(): pl.pallas_call(step_kernel, out_shape=(jax.ShapeDtypeStruct(velocity.shap...  38.7 us

profile of v7, /device:TPU:1, one launch (start us, length us, event | category | flops | bytes accessed | tf_op | source)
XLA Modules:
  0.0 40.1 jit_solution(17442363664836277651)
XLA Ops:
  0.6 38.7 %shard_map.86 = (f32[3,1,256,128]{3,2,1,0:T(8,128)S(1)}, f32[1,256,128]{2,1,0:T(8,128)S(1)}) custom-call(f32[2,64]{1,0:T(2,128)} %faces.1, f32[3,1,256,128]{3,2,1,0:T(8,128)} %velocity_in.1, bf16[3,1,256,128]{3,2,1,0:T(8,128)(2,1)} %earlier_in.1, bf16[2,256,256]{2,1,0:T(8,128)(2,1)} %constant.8.clone.y_second_in, ...), custom_call_target="tpu_custom_call" | custom-call | tf_op jit(solution)/shard_map/pallas_call | solution.py:515
  39.3 0.8 %shard_map.87 = (f32[3,1,256,128]{3,2,1,0:T(8,128)}, f32[1,256,128]{2,1,0:T(8,128)}) custom-call(f32[3,1,256,128]{3,2,1,0:T(8,128)S(1)} %get-tuple-element.4.step_in, f32[1,256,128]{2,1,0:T(8,128)S(1)} %get-tuple-element.5.pressure_in), custom_call_target="tpu_custom_call" | custom-call | tf_op jit(solution)/shard_map/pallas_call | solution.py:561
